TPU v7x, 256 devices: a whole 4x4x8 slice. The times are simulated.
256 devices in a mesh: row: 32 (over z, y), feat: 8 (over x, core).
Axes of the slice: x: 4, y: 4, z: 8, core: 2. Of those that a mesh axis runs over, the one named last changes fastest.
Arguments:
- design: bfloat16 [4096, 65536], P('row', 'feat'), may hold values from -0.0234375 to 0.0234375
- targets: bfloat16 [4096, 48], P('row'), may hold values from -6 to 6
- factor: float32 [65536, 256], P(('feat', 'row')), may hold values from -0.09375 to 0.09375
- weights: float32 [256], replicated, may hold values from 0.3 to 3
- penalty: float32 [48], replicated, may hold values from 0.05 to 0.5
Outputs:
- solution: float32 [65536, 48], P(('feat', 'row'))
- residual: float32 [65536, 48], P(('feat', 'row'))
All inputs are finite; a program needn't handle non-finite values.
Results may differ from a plain program's by a relative error of at most 0.024.
Values may be sent and summed in bfloat16 or wider, within the bound.
No kernel may reach another device: no remote copies, remote signals or barrier semaphores. Data moves between devices by JAX's collectives and lax.ppermute only.
A program may use at most 64 MiB of HBM per device.

v0:
```python
import jax
import jax.numpy as jnp
from jax import lax
from jax.experimental import pallas as pl
from jax.experimental.pallas import tpu as pltpu
from jax.sharding import Mesh
from jax.sharding import PartitionSpec as P


ITERS = 3
ROW = ("zh", "zl", "y")
FEAT = ("x", "c")
OWN = ("zl", "y")
MANY = ("zl", "y", "x", "c")
N_MANY, N_ZH = 64, 4
T, RANK, BLOCK = 48, 256, 1024
SCAL = 480
HEAD = 512
BF = jnp.bfloat16
F32 = jnp.float32


def exchange(pieces, axes):
    return lax.all_to_all(pieces, axes, 0, 0, tiled=True)


def dot(a, b):
    return jnp.dot(a, b, preferred_element_type=F32)


def dot_t(a, b):
    return lax.dot_general(a, b, (((1,), (1,)), ((), ())), preferred_element_type=F32)


PARAMS = pltpu.CompilerParams(vmem_limit_bytes=20 * 1024 * 1024)


IN_HBM = pl.BlockSpec(memory_space=pltpu.HBM)
IN_VMEM = pl.BlockSpec(memory_space=pltpu.VMEM)
IN_SMEM = pl.BlockSpec(memory_space=pltpu.SMEM)


def call(body, out):
    return pl.pallas_call(body, out_shape=out, compiler_params=PARAMS)


def fetch(pairs, sems):
    copies = [pltpu.make_async_copy(a, b, sems.at[i]) for i, (a, b) in enumerate(pairs)]
    for copy in copies:
        copy.start()
    return copies


def shape(*dims, dtype=F32):
    return jax.ShapeDtypeStruct(dims, dtype)


def columns(parts):
    lane = lax.broadcasted_iota(jnp.int32, (T, 128), 1)
    block = jnp.zeros((T, 128), F32)
    for index, part in enumerate(parts):
        block = jnp.where(lane == index, part, block)
    return block


def split16(value):
    high = value.astype(BF).astype(F32)
    return high, value - high


def total_of(array):
    return jnp.sum(array, axis=1, keepdims=True)


CHUNKS, DEEP = 4, 32


def pack_kernel(design, goal, out, rows, packed, goals, sems):
    def inward(index):
        at = pl.ds(index * DEEP, DEEP)
        return pltpu.make_async_copy(design.at[at, :], rows.at[at, :], sems.at[index])

    def outward(index):
        at = pl.ds(index * DEEP, DEEP)
        return pltpu.make_async_copy(
            packed.at[:, at, :], out.at[:, at, :], sems.at[CHUNKS + index]
        )

    for index in range(CHUNKS):
        inward(index).start()
    for to in range(8):
        for index in range(6):
            goals[to, :, index * 128 : (index + 1) * 128] = goal[index * 8 : index * 8 + 8, :]
        goals[to, :, 768:] = jnp.zeros((8, 256), BF)
    last = pltpu.make_async_copy(goals, out.at[:, 128:136, :], sems.at[2 * CHUNKS])
    last.start()
    for index in range(CHUNKS):
        inward(index).wait()
        low, high = index * DEEP, (index + 1) * DEEP
        for to in range(8):
            for part in range(4):
                at = (part * 8 + to) * 256
                packed[to, low:high, part * 256 : (part + 1) * 256] = rows[low:high, at : at + 256]
        outward(index).start()
    for index in range(CHUNKS):
        outward(index).wait()
    last.wait()


def pack(design, goal):
    return pl.pallas_call(
        pack_kernel,
        out_shape=shape(8, 136, BLOCK, dtype=BF),
        in_specs=[IN_HBM, IN_VMEM],
        out_specs=IN_HBM,
        scratch_shapes=[
            pltpu.VMEM((128, 8192), BF),
            pltpu.VMEM((8, 128, BLOCK), BF),
            pltpu.VMEM((8, 8, BLOCK), BF),
            pltpu.SemaphoreType.DMA((2 * CHUNKS + 1,)),
        ],
    )(design, goal)


def start_kernel(mat, zh, *outs):
    part = jnp.zeros((T, BLOCK), F32)
    for src in range(8):
        goal = jnp.concatenate(
            [mat[src, 128:136, t * 128 : (t + 1) * 128].astype(F32) for t in range(6)], axis=0
        ).astype(BF)
        part = part + dot(goal, mat[src, :128, :])
    high, low = split16(part)
    for shift, out in enumerate(outs):
        out[:, :BLOCK] = high.astype(BF)
        out[:, BLOCK:] = own_part(low, lax.rem(zh[0] + shift, N_ZH)).astype(BF)


def start(mat, zh):
    return pl.pallas_call(
        start_kernel,
        out_shape=(shape(T, BLOCK + 256, dtype=BF),) * N_ZH,
        in_specs=[IN_VMEM, IN_SMEM],
        compiler_params=PARAMS,
    )(mat, zh)


def cross_kernel(mat, fac, out):
    factor = fac[...]
    both = jnp.zeros((RANK, RANK), F32)
    for index in range(4):
        rows = fac[index * 256 : (index + 1) * 256, :]
        both = both + lax.dot_general(
            rows, rows, (((0,), (0,)), ((), ())), preferred_element_type=F32
        )
    both = both.astype(BF)
    for src in range(8):
        block = dot(mat[src, :128, :], factor).astype(BF)
        for half in range(2):
            for part in range(4):
                rows = block[part * 32 : (part + 1) * 32, half * 128 : (half + 1) * 128]
                out[src * 8 + half * 4 + part, :32, :] = rows
    for half in range(2):
        for part in range(32):
            rows = both[part * 8 : (part + 1) * 8, half * 128 : (half + 1) * 128]
            out[half * 32 + part, 32:40, :] = rows


def write_head(residual, direction, mat, fac, out):
    low = residual.astype(BF)
    for src in range(8):
        out[src * T : (src + 1) * T, :] = dot_t(low, mat[src, :128, :]).astype(BF)
    seen = dot(low, fac[...]).astype(BF)
    out[384:432, :] = seen[:, :128]
    out[432:480, :] = seen[:, 128:]
    rr = split16(total_of(residual * residual))
    rd = split16(total_of(residual * direction))
    block = jnp.concatenate([columns([*rr, *rd]), jnp.zeros((80, 128), F32)], axis=0)
    tile = block.T[:32, :]
    out[SCAL:HEAD, :] = tile.astype(BF)


def first_kernel(a0, a1, a2, a3, mat, fac, out, start_out, held, sem):
    total = a0[...].astype(F32)
    for other in (a1, a2, a3):
        total = total + other[...].astype(F32)
    held[...] = total
    store = pltpu.make_async_copy(held, start_out, sem.at[0])
    store.start()
    residual = total[:, :BLOCK]
    write_head(residual, residual, mat, fac, out)
    store.wait()


def first_call(arrived, mat, fac):
    return pl.pallas_call(
        first_kernel,
        out_shape=(shape(HEAD, 128, dtype=BF), shape(T, BLOCK + 256)),
        in_specs=[IN_VMEM] * 6,
        out_specs=(IN_VMEM, IN_HBM),
        scratch_shapes=[pltpu.VMEM((T, BLOCK + 256), F32), pltpu.SemaphoreType.DMA((1,))],
        compiler_params=PARAMS,
    )(*arrived, mat, fac)


def own_part(array, zh):
    mine = array[:, :256]
    for index in range(1, N_ZH):
        mine = jnp.where(zh == index, array[:, index * 256 : (index + 1) * 256], mine)
    return mine


D_AT, R_AT, S_AT, C_AT, WIDE = 0, BLOCK, 2 * BLOCK, 2 * BLOCK + RANK, 2 * BLOCK + RANK + 128


def next_kernel(more, arrived, zh, penalty, mat, state, residual_in, fac_in, *refs):
    refs = list(refs)
    answer_in = refs.pop(0) if more else None
    out, residual_out, answer_out, direction_v, scal_v, residual_v, fac_v, answer_v, sems = refs
    copies = fetch(
        [
            (state.at[:, D_AT:R_AT], direction_v),
            (state.at[:, C_AT:WIDE], scal_v),
            (residual_in.at[:, :BLOCK], residual_v),
            (fac_in, fac_v),
        ]
        + ([(answer_in, answer_v)] if more else []),
        sems,
    )
    hess = jnp.zeros((T, BLOCK + 128), F32)
    for source in range(N_ZH):
        hess = hess + arrived[source].astype(F32)
    square = hess[:, BLOCK : BLOCK + 1] + hess[:, BLOCK + 1 : BLOCK + 2]
    hess = hess[:, :BLOCK]
    ridge = penalty[:, :1]
    for copy in copies[:3]:
        copy.wait()
    inner, dd = scal_v[:, :1], scal_v[:, 1:2]
    direction = direction_v[...]
    step = inner / (square + ridge * dd)
    residual = residual_v[...] - step * (hess + ridge * direction)
    residual_v[...] = residual
    answer = step * own_part(direction, zh[0])
    if more:
        copies[4].wait()
        answer = answer_v[...] + answer
    answer_v[...] = answer
    stores = [
        pltpu.make_async_copy(residual_v, residual_out, sems.at[5]),
        pltpu.make_async_copy(answer_v, answer_out, sems.at[6]),
    ]
    for copy in stores:
        copy.start()
    copies[3].wait()
    write_head(residual, direction, mat, fac_v, out)
    for copy in stores:
        copy.wait()


def next_call(arrived, zh, ridge, mat, state, residual, fac, answer):
    more = answer is not None
    extra = (answer,) if more else ()
    return pl.pallas_call(
        lambda *refs: next_kernel(more, *refs),
        out_shape=(shape(HEAD, 128, dtype=BF), shape(T, BLOCK), shape(T, 256)),
        in_specs=[IN_VMEM, IN_SMEM, IN_VMEM, IN_VMEM] + [IN_HBM] * (3 + len(extra)),
        out_specs=(IN_VMEM, IN_HBM, IN_HBM),
        scratch_shapes=[
            pltpu.VMEM((T, BLOCK), F32),
            pltpu.VMEM((T, 128), F32),
            pltpu.VMEM((T, BLOCK), F32),
            pltpu.VMEM((BLOCK, RANK), BF),
            pltpu.VMEM((T, 256), F32),
            pltpu.SemaphoreType.DMA((7,)),
        ],
        compiler_params=PARAMS,
    )(arrived, zh, ridge, mat, state, residual, fac, *extra)


def search_kernel(first, last, back, zh, weights, mat, residual_in, fac_in, *refs):
    refs = list(refs)
    state_in = None if first else refs.pop(0)
    full = back if first else refs.pop(0)
    answer_in, fix_in = (refs.pop(0), refs.pop(0)) if last else (None, None)
    out, state_out, residual_v, fac_v, sems, state_v = refs[:6]
    refs = refs[6:]

    def lanes(array, low, high):
        return array.at[:, low:high]

    pairs = [(residual_in.at[:, :BLOCK], residual_v), (fac_in, fac_v)]
    if not first:
        full_v = refs.pop(0)
        pairs = [
            (full, full_v),
            (lanes(state_in, S_AT, WIDE), lanes(state_v, S_AT, WIDE)),
            (lanes(state_in, R_AT, S_AT), lanes(state_v, R_AT, S_AT)),
            (lanes(state_in, D_AT, R_AT), lanes(state_v, D_AT, R_AT)),
        ] + pairs
        full = full_v
    late = 0 if first else 3
    if last:
        answer_v, fix_v, tail_v = refs
        pairs += [(answer_in, answer_v), (fix_in.at[:, BLOCK:], fix_v)]
    copies = fetch(pairs, sems)

    def head(tile, count):
        if first:
            return jnp.concatenate(
                [back[t, 40:48, :].astype(F32) for t in range(tile, tile + count)], axis=0
            )
        return back[tile * 8 : (tile + count) * 8, :].astype(F32)

    def crossed(src, half):
        at = src * 8 + half * 4
        return full[at : at + 4, :32, :].reshape(128, 128)

    def grammed(half):
        return full[half * 32 : half * 32 + 32, 32:40, :].astype(F32).reshape(256, 128).astype(BF)

    projected = jnp.concatenate([head(48, 6), head(54, 6)], axis=1)
    tile = jnp.concatenate([head(60, 1), jnp.zeros((120, 128), F32)], axis=0).T
    rr = tile[:T, 0:1] + tile[:T, 1:2]
    rd = tile[:T, 2:3] + tile[:T, 3:4]
    scaled = weights[0:1, :] * projected
    cross_inner = total_of(scaled * projected)
    inner = rr + cross_inner
    low = scaled.astype(BF)
    if not first:
        for copy in copies[:late]:
            copy.wait()
        beta = inner / state_v[:, C_AT : C_AT + 1]
    row_lows = []
    square = jnp.zeros((T, 1), F32)
    for src in range(8):
        row = head(src * 6, 6) + dot_t(low[:, :128], crossed(src, 0))
        row = row + dot_t(low[:, 128:], crossed(src, 1))
        at = R_AT + src * 128
        if not first:
            row = row + beta * state_v[:, at : at + 128]
        state_v[:, at : at + 128] = row
        row_low = row.astype(BF)
        square = square + total_of(row * row_low.astype(F32))
        row_lows.append(row_low)
    through = jnp.concatenate([dot(low, grammed(0)), dot(low, grammed(1))], axis=1)
    dd = rr + 2.0 * cross_inner + total_of(scaled * through)
    seen = projected + through
    if not first:
        sd = rd + total_of(scaled * state_v[:, S_AT:C_AT])
        dd = dd + 2.0 * beta * sd + beta * beta * state_v[:, C_AT + 1 : C_AT + 2]
        seen = seen + beta * state_v[:, S_AT:C_AT]
    for copy in copies[late:]:
        copy.wait()
    direction = residual_v[...] + dot_t(low, fac_v[...])
    if not first:
        direction = direction + beta * state_v[:, D_AT:R_AT]
    if last:
        tail_v[:, :256] = own_part(direction, zh[0])
        tail_v[:, 256:512] = answer_v[...]
        tail_v[:, 512:768] = own_part(residual_v[...], zh[0]) + fix_v[...]
        tail_v[:, 768:] = columns([inner, dd])
        store = pltpu.make_async_copy(tail_v, state_out, sems.at[8])
    else:
        state_v[:, D_AT:R_AT] = direction
        state_v[:, S_AT:C_AT] = seen
        state_v[:, C_AT:WIDE] = columns([inner, dd])
        store = pltpu.make_async_copy(state_v, state_out, sems.at[8])
    store.start()
    part = jnp.zeros((T, BLOCK), F32)
    for src in range(8):
        part = part + dot(row_lows[src], mat[src, :128, :])
    extra = columns(split16(square)).astype(BF)
    high, low = split16(part)
    high, low = high.astype(BF), low.astype(BF)
    for to in range(N_ZH):
        if last:
            mine = slice(to * 256, (to + 1) * 256)
            out[to, :, :256] = high[:, mine]
            out[to, :, 256:512] = low[:, mine]
            out[to, :, 512:] = extra
        else:
            out[to, :, :BLOCK] = high
            out[to, :, BLOCK:] = extra
    store.wait()


def search_call(first, last, back, zh, weights, mat, residual, fac, state, full, answer, fix):
    hbm = [residual, fac]
    if not first:
        hbm += [state, full]
    if last:
        hbm += [answer, fix]
    scratch = [
        pltpu.VMEM((T, BLOCK), F32),
        pltpu.VMEM((BLOCK, RANK), BF),
        pltpu.SemaphoreType.DMA((9,)),
        pltpu.VMEM((T, WIDE), F32),
    ]
    if not first:
        scratch.append(pltpu.VMEM((N_MANY, 48, 128), BF))
    if last:
        scratch += [pltpu.VMEM((T, 256), F32), pltpu.VMEM((T, 256), F32), pltpu.VMEM((T, 896), F32)]
    return pl.pallas_call(
        lambda *refs: search_kernel(first, last, *refs),
        out_shape=(
            shape(N_ZH, T, 640 if last else BLOCK + 128, dtype=BF),
            shape(T, 896 if last else WIDE),
        ),
        in_specs=[IN_VMEM, IN_SMEM, IN_VMEM, IN_VMEM] + [IN_HBM] * len(hbm),
        out_specs=(IN_VMEM, IN_HBM),
        scratch_shapes=scratch,
        compiler_params=PARAMS,
    )(back, zh, weights, mat, *hbm)


def middle_kernel(pieces, me, *refs):
    cross, out = refs if len(refs) == 2 else (None, *refs)
    tile = jnp.zeros((8, 128), F32)
    for source in range(N_MANY):
        tile = tile + pieces[source].astype(F32)
    high_a, low_a = split16(tile[0:1] + tile[1:2])
    high_b, low_b = split16(tile[2:3] + tile[3:4])
    line = lax.broadcasted_iota(jnp.int32, (8, 128), 0)
    again = tile
    for index, value in enumerate((high_a, low_a, high_b, low_b)):
        again = jnp.where(line == index, value, again)
    tile = jnp.where(me[0] == SCAL // 8, again, tile)
    if cross is not None:
        total = jnp.zeros((40, 128), F32)
        for source in range(N_MANY):
            total = total + cross[source].astype(F32)
        tile = jnp.concatenate([total, tile], axis=0)
    tile = tile.astype(BF)
    for target in range(N_MANY):
        out[target] = tile


def middle(pieces, me, cross=None):
    extra = () if cross is None else (cross,)
    return pl.pallas_call(
        middle_kernel,
        out_shape=shape(N_MANY, 48 if extra else 8, 128, dtype=BF),
        in_specs=[IN_VMEM, IN_SMEM] + [IN_VMEM] * len(extra),
        out_specs=IN_VMEM,
        compiler_params=PARAMS,
    )(pieces, me, *extra)


def final_kernel(arrived, tail, penalty, answer_out, residual_out):
    total = jnp.zeros((T, 640), F32)
    for source in range(N_ZH):
        total = total + arrived[source].astype(F32)
    square = total[:, 512:513] + total[:, 513:514]
    ridge = penalty[:, :1]
    mine = tail[:, :256]
    step = tail[:, 768:769] / (square + ridge * tail[:, 769:770])
    hess = total[:, :256] + total[:, 256:512] + ridge * mine
    answer_out[...] = tail[:, 256:512] + step * mine
    residual_out[...] = tail[:, 512:768] - step * hess


def program(design, targets, factor, weights, penalty):
    zh = lax.axis_index("zh")
    me = lax.axis_index(MANY).reshape(1)
    low_factor = factor.astype(BF)
    slots = jnp.zeros((N_ZH, 256, RANK), BF)
    slots = lax.dynamic_update_slice(slots, low_factor[None], (zh, 0, 0))
    for shift in range(1, N_ZH):
        pairs = [(i, (i + shift) % N_ZH) for i in range(N_ZH)]
        other = lax.ppermute(low_factor, "zh", pairs)
        slots = lax.dynamic_update_slice(slots, other[None], ((zh - shift) % N_ZH, 0, 0))
    fac = slots.reshape(BLOCK, RANK)

    spot = zh.reshape(1)
    mat = exchange(pack(design, targets.T), OWN)
    arrived = list(start(mat, spot))
    for shift in range(1, N_ZH):
        pairs = [(i, (i + shift) % N_ZH) for i in range(N_ZH)]
        arrived[shift] = lax.ppermute(arrived[shift], "zh", pairs)
    cross = call(cross_kernel, shape(N_MANY, 40, 128, dtype=BF))(mat, fac)
    cross = exchange(cross, MANY)

    w = jnp.broadcast_to(weights[None, :], (8, RANK))
    ridge = jnp.broadcast_to(penalty[:, None], (T, 128))

    packed, residual = first_call(arrived, mat, fac)
    packed, cross = lax.optimization_barrier((packed, cross))
    fix = residual
    answer = state = full = None
    for step_index in range(ITERS):
        first, last = step_index == 0, step_index == ITERS - 1
        pieces = exchange(packed.reshape(N_MANY, 8, 128), MANY)
        back = exchange(middle(pieces, me, cross if first else None), MANY)
        if first:
            full = back
        else:
            back = back.reshape(HEAD, 128)
        send, state = search_call(
            first, last, back, spot, w, mat, residual, fac, state, full, answer, fix
        )
        arrived = exchange(send, "zh")
        if not last:
            packed, residual, answer = next_call(
                arrived, spot, ridge, mat, state, residual, fac, answer
            )
    answer, residual = call(final_kernel, (shape(T, 256), shape(T, 256)))(arrived, state, ridge)
    return answer.T, residual.T


def solution(mesh):
    finer = Mesh(mesh.devices.reshape(4, 2, 4, 4, 2), ("zh", "zl", "y", "x", "c"))
    spec = P((*FEAT, *ROW), None)
    in_specs = (P(ROW, FEAT), P(ROW, None), spec, P(), P())
    return jax.shard_map(
        program, mesh=finer, in_specs=in_specs, out_specs=(spec, spec), check_vma=False
    )
```

profile of v0, /device:TPU:1, one launch (start us, length us, event | category | flops | bytes accessed | tf_op | source)
XLA Modules:
  0.0 232.3 jit_solution(6617349955609691252)
XLA Ops:
  0.6 3.3 %shard_map.68 = bf16[8,136,1024]{2,1,0:T(8,128)(2,1)} custom-call(bf16[128,8192]{1,0:T(8,128)(2,1)} %design.1, bf16[48,128]{1,0:T(8,128)(2,1)} %bitcast.31), custom_call_target="tpu_custom_call" | custom-call | tf_op jit(solution)/shard_map/pallas_call | solution.py:111
  3.9 0.0 copy-start.4
  3.9 6.5 %all-to-all-start = ((bf16[8,136,1024]{2,1,0:T(8,128)(2,1)}), bf16[8,136,1024]{2,1,0:T(8,128)(2,1)S(1)}, u32[]{:S(2)}, u32[]{:S(2)}) async-start(bf16[8,136,1024]{2,1,0:T(8,128)(2,1)} %shard_map.68), calls=%async_computation | async-start | bytes 4456448 | tf_op jit(solution)/shard_map/all_to_all | solution.py:24
  10.5 0.0 copy-done.4
  10.5 3.1 %collective-permute-start.3 = (bf16[256,256]{1,0:T(8,128)(2,1)S(1)}, bf16[256,256]{1,0:T(8,128)(2,1)S(1)}, u32[]{:S(2)}, u32[]{:S(2)}) collective-permute-start(bf16[256,256]{1,0:T(8,128)(2,1)S(1)} %get-tuple-element.47), channel_id=1, source_target_pairs={{0,64},{64,128},{128,192},{192,0},{1,65},{65,129},{129,193},{193,1... | collective-permute-start | bytes 393224 | tf_op jit(solution)/shard_map/ppermute | solution.py:469
  13.6 4.2 %collective-permute-start.4 = (bf16[256,256]{1,0:T(8,128)(2,1)S(1)}, bf16[256,256]{1,0:T(8,128)(2,1)S(1)}, u32[]{:S(2)}, u32[]{:S(2)}) collective-permute-start(bf16[256,256]{1,0:T(8,128)(2,1)S(1)} %get-tuple-element.47), channel_id=1, source_target_pairs={{0,128},{64,192},{128,0},{192,64},{1,129},{65,193},{129,1},{193,65... | collective-permute-start | bytes 393224 | tf_op jit(solution)/shard_map/ppermute | solution.py:469
  17.8 2.4 %collective-permute-start.5 = (bf16[256,256]{1,0:T(8,128)(2,1)S(1)}, bf16[256,256]{1,0:T(8,128)(2,1)S(1)}, u32[]{:S(2)}, u32[]{:S(2)}) collective-permute-start(bf16[256,256]{1,0:T(8,128)(2,1)S(1)} %get-tuple-element.47), channel_id=1, source_target_pairs={{0,192},{64,0},{128,64},{192,128},{1,193},{65,1},{129,65},{193,129... | collective-permute-start | bytes 393224 | tf_op jit(solution)/shard_map/ppermute | solution.py:469
  20.2 25.3 %collective-permute-done.3 = bf16[256,256]{1,0:T(8,128)(2,1)S(1)} collective-permute-done((bf16[256,256]{1,0:T(8,128)(2,1)S(1)}, bf16[256,256]{1,0:T(8,128)(2,1)S(1)}, u32[]{:S(2)}, u32[]{:S(2)}) %collective-permute-start.3) | collective-permute-done | bytes 131104 | tf_op jit(solution)/shard_map/ppermute | solution.py:469
  45.5 3.8 %collective-permute-done.4 = bf16[256,256]{1,0:T(8,128)(2,1)S(1)} collective-permute-done((bf16[256,256]{1,0:T(8,128)(2,1)S(1)}, bf16[256,256]{1,0:T(8,128)(2,1)S(1)}, u32[]{:S(2)}, u32[]{:S(2)}) %collective-permute-start.4) | collective-permute-done | bytes 131104 | tf_op jit(solution)/shard_map/ppermute | solution.py:469
  49.4 0.0 collective-permute-done.5
  49.4 0.0 all-to-all-done.mat.refs_3_
  49.4 0.9 shard_map.71
  50.3 0.0 copy-start
  50.3 0.8 copy-done
  51.1 10.3 %all-to-all-start.1 = ((bf16[64,40,128]{2,1,0:T(8,128)(2,1)}), bf16[64,40,128]{2,1,0:T(8,128)(2,1)S(1)}, u32[]{:S(2)}, u32[]{:S(2)}) async-start(bf16[64,40,128]{2,1,0:T(8,128)(2,1)} %copy-done), calls=%async_computation.1 | async-start | bytes 1310720 | tf_op jit(solution)/shard_map/all_to_all | solution.py:24
  61.5 0.4 shard_map.69
  61.9 2.7 %collective-permute-start = (bf16[48,1280]{1,0:T(8,128)(2,1)S(1)}, bf16[48,1280]{1,0:T(8,128)(2,1)S(1)}, u32[]{:S(2)}, u32[]{:S(2)}) collective-permute-start(bf16[48,1280]{1,0:T(8,128)(2,1)S(1)} %get-tuple-element.25), channel_id=1, source_target_pairs={{0,64},{64,128},{128,192},{192,0},{1,65},{65,129},{129,193},{193,1... | collective-permute-start | bytes 368648 | tf_op jit(solution)/shard_map/ppermute | solution.py:478
  64.6 1.2 collective-permute-start.1
  65.8 3.2 %collective-permute-start.2 = (bf16[48,1280]{1,0:T(8,128)(2,1)S(1)}, bf16[48,1280]{1,0:T(8,128)(2,1)S(1)}, u32[]{:S(2)}, u32[]{:S(2)}) collective-permute-start(bf16[48,1280]{1,0:T(8,128)(2,1)S(1)} %get-tuple-element.27), channel_id=1, source_target_pairs={{0,192},{64,0},{128,64},{192,128},{1,193},{65,1},{129,65},{193,129... | collective-permute-start | bytes 368648 | tf_op jit(solution)/shard_map/ppermute | solution.py:478
  69.0 7.0 %collective-permute-done.a1 = bf16[48,1280]{1,0:T(8,128)(2,1)S(1)} collective-permute-done((bf16[48,1280]{1,0:T(8,128)(2,1)S(1)}, bf16[48,1280]{1,0:T(8,128)(2,1)S(1)}, u32[]{:S(2)}, u32[]{:S(2)}) %collective-permute-start) | collective-permute-done | bytes 122912 | tf_op jit(solution)/shard_map/ppermute | solution.py:478
  76.0 4.4 %collective-permute-done.1.a2 = bf16[48,1280]{1,0:T(8,128)(2,1)S(1)} collective-permute-done((bf16[48,1280]{1,0:T(8,128)(2,1)S(1)}, bf16[48,1280]{1,0:T(8,128)(2,1)S(1)}, u32[]{:S(2)}, u32[]{:S(2)}) %collective-permute-start.1) | collective-permute-done | bytes 122912 | tf_op jit(solution)/shard_map/ppermute | solution.py:478
  80.4 0.0 collective-permute-done.2.a3
  80.4 1.3 shard_map.70
  81.7 0.0 copy-start.1
  81.7 0.7 copy-done.1
  82.4 0.7 copy-done.3
  83.0 0.0 all-to-all-done.1.refs_0_
  83.0 11.4 %all-to-all-start.2 = ((bf16[64,8,128]{2,1,0:T(8,128)(2,1)}), bf16[64,8,128]{2,1,0:T(8,128)(2,1)S(1)}, u32[]{:S(2)}, u32[]{:S(2)}) async-start(bf16[64,8,128]{2,1,0:T(8,128)(2,1)} %bitcast.28), calls=%async_computation.2 | async-start | bytes 262144 | tf_op jit(solution)/shard_map/all_to_all | solution.py:24
  94.4 8.5 %all-to-all-done.2.pieces = bf16[64,8,128]{2,1,0:T(8,128)(2,1)S(1)} async-done(((bf16[64,8,128]{2,1,0:T(8,128)(2,1)}), bf16[64,8,128]{2,1,0:T(8,128)(2,1)S(1)}, u32[]{:S(2)}, u32[]{:S(2)}) %all-to-all-start.2) | async-done | bytes 131104 | tf_op jit(solution)/shard_map/all_to_all | solution.py:24
  102.9 0.2 shard_map.72
  103.1 18.9 %all_to_all.55.refs_0_.refs_7_ = bf16[64,48,128]{2,1,0:T(8,128)(2,1)S(1)} all-to-all(bf16[64,48,128]{2,1,0:T(8,128)(2,1)S(1)} %shard_map.72), channel_id=1, replica_groups=mesh['zh'=4,'zl'=2,'y'=4,'x'=4,'c'=2] {'zl','y','x','c'}, dimensions={0} | all-to-all | bytes 1572864 | tf_op jit(solution)/shard_map/all_to_all | solution.py:24
  121.9 0.0 copy-done.5
  122.0 1.7 shard_map.73
  123.7 17.3 %all_to_all.56.refs_0_ = bf16[4,48,1152]{2,1,0:T(8,128)(2,1)S(1)} all-to-all(bf16[4,48,1152]{2,1,0:T(8,128)(2,1)S(1)} %get-tuple-element.32), channel_id=1, replica_groups=mesh['zh'=4,'zl'=2,'y'=4,'x'=4,'c'=2] {'zh'}, dimensions={0} | all-to-all | bytes 884736 | tf_op jit(solution)/shard_map/all_to_all | solution.py:24
  141.0 0.1 broadcast_in_dim.33.refs_2_.penalty
  141.1 1.6 shard_map.74
  142.7 14.6 %all_to_all.57.pieces = bf16[64,8,128]{2,1,0:T(8,128)(2,1)S(1)} all-to-all(bf16[64,8,128]{2,1,0:T(8,128)(2,1)S(1)} %bitcast.30), channel_id=1, replica_groups=mesh['zh'=4,'zl'=2,'y'=4,'x'=4,'c'=2] {'zl','y','x','c'}, dimensions={0} | all-to-all | bytes 262144 | tf_op jit(solution)/shard_map/all_to_all | solution.py:24
  157.3 0.1 shard_map.75
  157.4 12.6 %all_to_all.58 = bf16[64,8,128]{2,1,0:T(8,128)(2,1)S(1)} all-to-all(bf16[64,8,128]{2,1,0:T(8,128)(2,1)S(1)} %shard_map.75), channel_id=1, replica_groups=mesh['zh'=4,'zl'=2,'y'=4,'x'=4,'c'=2] {'zl','y','x','c'}, dimensions={0} | all-to-all | bytes 262144 | tf_op jit(solution)/shard_map/all_to_all | solution.py:24
  170.0 2.2 shard_map.76
  172.2 16.0 %all_to_all.59.refs_0_ = bf16[4,48,1152]{2,1,0:T(8,128)(2,1)S(1)} all-to-all(bf16[4,48,1152]{2,1,0:T(8,128)(2,1)S(1)} %get-tuple-element.36), channel_id=1, replica_groups=mesh['zh'=4,'zl'=2,'y'=4,'x'=4,'c'=2] {'zh'}, dimensions={0} | all-to-all | bytes 884736 | tf_op jit(solution)/shard_map/all_to_all | solution.py:24
  188.2 1.9 shard_map.77
  190.2 14.9 %all_to_all.60.pieces = bf16[64,8,128]{2,1,0:T(8,128)(2,1)S(1)} all-to-all(bf16[64,8,128]{2,1,0:T(8,128)(2,1)S(1)} %bitcast.29), channel_id=1, replica_groups=mesh['zh'=4,'zl'=2,'y'=4,'x'=4,'c'=2] {'zl','y','x','c'}, dimensions={0} | all-to-all | bytes 262144 | tf_op jit(solution)/shard_map/all_to_all | solution.py:24
  205.0 0.1 shard_map.78
  205.1 12.6 %all_to_all.61 = bf16[64,8,128]{2,1,0:T(8,128)(2,1)S(1)} all-to-all(bf16[64,8,128]{2,1,0:T(8,128)(2,1)S(1)} %shard_map.78), channel_id=1, replica_groups=mesh['zh'=4,'zl'=2,'y'=4,'x'=4,'c'=2] {'zl','y','x','c'}, dimensions={0} | all-to-all | bytes 262144 | tf_op jit(solution)/shard_map/all_to_all | solution.py:24
  217.7 2.3 shard_map.79
  220.0 11.5 %all_to_all.62.arrived = bf16[4,48,640]{2,1,0:T(8,128)(2,1)S(1)} all-to-all(bf16[4,48,640]{2,1,0:T(8,128)(2,1)S(1)} %get-tuple-element.42), channel_id=1, replica_groups=mesh['zh'=4,'zl'=2,'y'=4,'x'=4,'c'=2] {'zh'}, dimensions={0} | all-to-all | bytes 491520 | tf_op jit(solution)/shard_map/all_to_all | solution.py:24
  231.5 0.8 shard_map.80
  (12 shorter events, 0.1 us)
Async XLA Ops:
  3.9 6.6 %copy-start.4 = (f32[256,256]{1,0:T(8,128)S(1)}, f32[256,256]{1,0:T(8,128)}, u32[]{:S(2)}) copy-start(f32[256,256]{1,0:T(8,128)} %param.7) | copy-start | bytes 786436
  3.9 45.5 %all-to-all-start = ((bf16[8,136,1024]{2,1,0:T(8,128)(2,1)}), bf16[8,136,1024]{2,1,0:T(8,128)(2,1)S(1)}, u32[]{:S(2)}, u32[]{:S(2)}) async-start(bf16[8,136,1024]{2,1,0:T(8,128)(2,1)} %shard_map.68), calls=%async_computation | async-start | bytes 4456448 | tf_op jit(solution)/shard_map/all_to_all | solution.py:24
  10.5 35.0 %collective-permute-start.3 = (bf16[256,256]{1,0:T(8,128)(2,1)S(1)}, bf16[256,256]{1,0:T(8,128)(2,1)S(1)}, u32[]{:S(2)}, u32[]{:S(2)}) collective-permute-start(bf16[256,256]{1,0:T(8,128)(2,1)S(1)} %get-tuple-element.47), channel_id=1, source_target_pairs={{0,64},{64,128},{128,192},{192,0},{1,65},{65,129},{129,193},{193,1... | collective-permute-start | bytes 393224 | tf_op jit(solution)/shard_map/ppermute | solution.py:469
  13.6 35.7 %collective-permute-start.4 = (bf16[256,256]{1,0:T(8,128)(2,1)S(1)}, bf16[256,256]{1,0:T(8,128)(2,1)S(1)}, u32[]{:S(2)}, u32[]{:S(2)}) collective-permute-start(bf16[256,256]{1,0:T(8,128)(2,1)S(1)} %get-tuple-element.47), channel_id=1, source_target_pairs={{0,128},{64,192},{128,0},{192,64},{1,129},{65,193},{129,1},{193,65... | collective-permute-start | bytes 393224 | tf_op jit(solution)/shard_map/ppermute | solution.py:469
  17.8 31.6 %collective-permute-start.5 = (bf16[256,256]{1,0:T(8,128)(2,1)S(1)}, bf16[256,256]{1,0:T(8,128)(2,1)S(1)}, u32[]{:S(2)}, u32[]{:S(2)}) collective-permute-start(bf16[256,256]{1,0:T(8,128)(2,1)S(1)} %get-tuple-element.47), channel_id=1, source_target_pairs={{0,192},{64,0},{128,64},{192,128},{1,193},{65,1},{129,65},{193,129... | collective-permute-start | bytes 393224 | tf_op jit(solution)/shard_map/ppermute | solution.py:469
  50.3 0.8 copy-start
  51.1 31.9 %all-to-all-start.1 = ((bf16[64,40,128]{2,1,0:T(8,128)(2,1)}), bf16[64,40,128]{2,1,0:T(8,128)(2,1)S(1)}, u32[]{:S(2)}, u32[]{:S(2)}) async-start(bf16[64,40,128]{2,1,0:T(8,128)(2,1)} %copy-done), calls=%async_computation.1 | async-start | bytes 1310720 | tf_op jit(solution)/shard_map/all_to_all | solution.py:24
  61.9 14.1 %collective-permute-start = (bf16[48,1280]{1,0:T(8,128)(2,1)S(1)}, bf16[48,1280]{1,0:T(8,128)(2,1)S(1)}, u32[]{:S(2)}, u32[]{:S(2)}) collective-permute-start(bf16[48,1280]{1,0:T(8,128)(2,1)S(1)} %get-tuple-element.25), channel_id=1, source_target_pairs={{0,64},{64,128},{128,192},{192,0},{1,65},{65,129},{129,193},{193,1... | collective-permute-start | bytes 368648 | tf_op jit(solution)/shard_map/ppermute | solution.py:478
  64.6 15.8 %collective-permute-start.1 = (bf16[48,1280]{1,0:T(8,128)(2,1)S(1)}, bf16[48,1280]{1,0:T(8,128)(2,1)S(1)}, u32[]{:S(2)}, u32[]{:S(2)}) collective-permute-start(bf16[48,1280]{1,0:T(8,128)(2,1)S(1)} %get-tuple-element.26), channel_id=1, source_target_pairs={{0,128},{64,192},{128,0},{192,64},{1,129},{65,193},{129,1},{193,65... | collective-permute-start | bytes 368648 | tf_op jit(solution)/shard_map/ppermute | solution.py:478
  65.8 14.6 %collective-permute-start.2 = (bf16[48,1280]{1,0:T(8,128)(2,1)S(1)}, bf16[48,1280]{1,0:T(8,128)(2,1)S(1)}, u32[]{:S(2)}, u32[]{:S(2)}) collective-permute-start(bf16[48,1280]{1,0:T(8,128)(2,1)S(1)} %get-tuple-element.27), channel_id=1, source_target_pairs={{0,192},{64,0},{128,64},{192,128},{1,193},{65,1},{129,65},{193,129... | collective-permute-start | bytes 368648 | tf_op jit(solution)/shard_map/ppermute | solution.py:478
  81.7 0.7 copy-start.1
  82.4 0.7 copy-start.3
  83.0 38.9 %copy-start.5 = (f32[256]{0:T(256)S(1)}, f32[256]{0:T(256)}, u32[]{:S(2)}) copy-start(f32[256]{0:T(256)} %param.8) | copy-start | bytes 3076
  83.0 19.9 %all-to-all-start.2 = ((bf16[64,8,128]{2,1,0:T(8,128)(2,1)}), bf16[64,8,128]{2,1,0:T(8,128)(2,1)S(1)}, u32[]{:S(2)}, u32[]{:S(2)}) async-start(bf16[64,8,128]{2,1,0:T(8,128)(2,1)} %bitcast.28), calls=%async_computation.2 | async-start | bytes 262144 | tf_op jit(solution)/shard_map/all_to_all | solution.py:24
  102.9 19.1 %copy-start.2 = (f32[48,1280]{1,0:T(8,128)S(1)}, f32[48,1280]{1,0:T(8,128)}, u32[]{:S(2)}) copy-start(f32[48,1280]{1,0:T(8,128)} %copy-done.1) | copy-start | bytes 737284
  122.0 19.0 %copy-start.6 = (f32[48]{0:T(128)S(1)}, f32[48]{0:T(128)}, u32[]{:S(2)}) copy-start(f32[48]{0:T(128)} %param.9) | copy-start | bytes 580
where the time goes:
time: 233 us; the launch traced here: 232 us
  blocking collectives  118 us (51%)
  waiting for transfers between devices  49 us (21%)
  starting transfers between devices  45 us (19%)
  Pallas kernels  16.8 us (7%)
  local copies, waits for them, and re-layouts  2.36 us (1%)
    all_to_all x8, blocking collectives, exchange(): return lax.all_to_all(pieces, axes, 0, 0, tiled=True)  118 us
    ppermute x3, waiting for transfers between devices, program(): other = lax.ppermute(low_factor, 'zh', pairs)  29.1 us
    all_to_all x3, starting transfers between devices, exchange(): return lax.all_to_all(pieces, axes, 0, 0, tiled=True)  28.2 us
    ppermute x3, waiting for transfers between devices, program(): arrived[shift] = lax.ppermute(arrived[shift], 'zh', pairs)  11.4 us
    ppermute x3, starting transfers between devices, program(): other = lax.ppermute(low_factor, 'zh', pairs)  9.66 us
    all_to_all x3, waiting for transfers between devices, exchange(): return lax.all_to_all(pieces, axes, 0, 0, tiled=True)  8.47 us
    ppermute x3, starting transfers between devices, program(): arrived[shift] = lax.ppermute(arrived[shift], 'zh', pairs)  7.07 us
    pallas_call x3, Pallas kernels, search_call(): pl.pallas_call(lambda *refs: search_kernel(first, last, *refs), out_shape...  6.21 us
  transfers between devices with their start and end apart: 9, of which 5 were waited for; matrix products, arithmetic and copies ran while one was open for 0% of the time, Pallas kernels for 1%

commit v1 on v0

--- a/solution.py
+++ b/solution.py
@@ -66,6 +66,16 @@
 def split16(value):
     high = value.astype(BF).astype(F32)
     return high, value - high
+
+
+def as_tile(column):
+    block = jnp.concatenate([columns(split16(column)), jnp.zeros((80, 128), F32)], axis=0)
+    return block.T[:8, :].astype(BF)
+
+
+def from_tile(tile):
+    block = jnp.concatenate([tile, jnp.zeros((120, 128), F32)], axis=0).T
+    return block[:T, 0:1] + block[:T, 1:2]
 
 
 def total_of(array):
@@ -122,7 +132,7 @@
     )(design, goal)
 
 
-def start_kernel(mat, zh, *outs):
+def start_kernel(mat, out):
     part = jnp.zeros((T, BLOCK), F32)
     for src in range(8):
         goal = jnp.concatenate(
@@ -130,18 +140,10 @@
         ).astype(BF)
         part = part + dot(goal, mat[src, :128, :])
     high, low = split16(part)
-    for shift, out in enumerate(outs):
-        out[:, :BLOCK] = high.astype(BF)
-        out[:, BLOCK:] = own_part(low, lax.rem(zh[0] + shift, N_ZH)).astype(BF)
-
-
-def start(mat, zh):
-    return pl.pallas_call(
-        start_kernel,
-        out_shape=(shape(T, BLOCK + 256, dtype=BF),) * N_ZH,
-        in_specs=[IN_VMEM, IN_SMEM],
-        compiler_params=PARAMS,
-    )(mat, zh)
+    high, low = high.astype(BF), low.astype(BF)
+    for to in range(N_ZH):
+        out[to, :, :BLOCK] = high
+        out[to, :, BLOCK:] = low[:, to * 256 : (to + 1) * 256]
 
 
 def cross_kernel(mat, fac, out):
@@ -165,41 +167,46 @@
             out[half * 32 + part, 32:40, :] = rows
 
 
-def write_head(residual, direction, mat, fac, out):
+def write_head(residual, direction, mat, fac, put):
     low = residual.astype(BF)
     for src in range(8):
-        out[src * T : (src + 1) * T, :] = dot_t(low, mat[src, :128, :]).astype(BF)
-    seen = dot(low, fac[...]).astype(BF)
-    out[384:432, :] = seen[:, :128]
-    out[432:480, :] = seen[:, 128:]
+        put(src * 6, dot_t(low, mat[src, :128, :]))
+    seen = dot(low, fac[...])
+    put(48, seen[:, :128])
+    put(54, seen[:, 128:])
     rr = split16(total_of(residual * residual))
     rd = split16(total_of(residual * direction))
     block = jnp.concatenate([columns([*rr, *rd]), jnp.zeros((80, 128), F32)], axis=0)
-    tile = block.T[:32, :]
-    out[SCAL:HEAD, :] = tile.astype(BF)
-
-
-def first_kernel(a0, a1, a2, a3, mat, fac, out, start_out, held, sem):
-    total = a0[...].astype(F32)
-    for other in (a1, a2, a3):
-        total = total + other[...].astype(F32)
+    put(60, block.T[:32, :])
+
+
+def first_kernel(arrived, mat, fac, cross, out, start_out, held, sem):
+    total = jnp.zeros((T, BLOCK + 256), F32)
+    for source in range(N_ZH):
+        total = total + arrived[source].astype(F32)
     held[...] = total
     store = pltpu.make_async_copy(held, start_out, sem.at[0])
     store.start()
+    out[:, :40, :] = cross[...]
+
+    def put(tile, rows):
+        for index in range(rows.shape[0] // 8):
+            out[tile + index, 40:48, :] = rows[index * 8 : index * 8 + 8, :].astype(BF)
+
     residual = total[:, :BLOCK]
-    write_head(residual, residual, mat, fac, out)
+    write_head(residual, residual, mat, fac, put)
     store.wait()
 
 
-def first_call(arrived, mat, fac):
+def first_call(arrived, mat, fac, cross):
     return pl.pallas_call(
         first_kernel,
-        out_shape=(shape(HEAD, 128, dtype=BF), shape(T, BLOCK + 256)),
-        in_specs=[IN_VMEM] * 6,
+        out_shape=(shape(N_MANY, 48, 128, dtype=BF), shape(T, BLOCK + 256)),
+        in_specs=[IN_VMEM] * 4,
         out_specs=(IN_VMEM, IN_HBM),
         scratch_shapes=[pltpu.VMEM((T, BLOCK + 256), F32), pltpu.SemaphoreType.DMA((1,))],
         compiler_params=PARAMS,
-    )(*arrived, mat, fac)
+    )(arrived, mat, fac, cross)
 
 
 def own_part(array, zh):
@@ -226,11 +233,11 @@
         + ([(answer_in, answer_v)] if more else []),
         sems,
     )
-    hess = jnp.zeros((T, BLOCK + 128), F32)
+    total = jnp.zeros((8 * T + 8, 128), F32)
     for source in range(N_ZH):
-        hess = hess + arrived[source].astype(F32)
-    square = hess[:, BLOCK : BLOCK + 1] + hess[:, BLOCK + 1 : BLOCK + 2]
-    hess = hess[:, :BLOCK]
+        total = total + arrived[source].astype(F32)
+    square = from_tile(total[8 * T :])
+    hess = jnp.concatenate([total[at * T : (at + 1) * T] for at in range(8)], axis=1)
     ridge = penalty[:, :1]
     for copy in copies[:3]:
         copy.wait()
@@ -251,7 +258,11 @@
     for copy in stores:
         copy.start()
     copies[3].wait()
-    write_head(residual, direction, mat, fac_v, out)
+
+    def put(tile, rows):
+        out[tile * 8 : tile * 8 + rows.shape[0], :] = rows.astype(BF)
+
+    write_head(residual, direction, mat, fac_v, put)
     for copy in stores:
         copy.wait()
 
@@ -368,18 +379,13 @@
     part = jnp.zeros((T, BLOCK), F32)
     for src in range(8):
         part = part + dot(row_lows[src], mat[src, :128, :])
-    extra = columns(split16(square)).astype(BF)
-    high, low = split16(part)
-    high, low = high.astype(BF), low.astype(BF)
+    part = part.astype(BF)
+    tile = as_tile(square)
     for to in range(N_ZH):
-        if last:
-            mine = slice(to * 256, (to + 1) * 256)
-            out[to, :, :256] = high[:, mine]
-            out[to, :, 256:512] = low[:, mine]
-            out[to, :, 512:] = extra
-        else:
-            out[to, :, :BLOCK] = high
-            out[to, :, BLOCK:] = extra
+        blocks = range(2 * to, 2 * to + 2) if last else range(8)
+        for index, at in enumerate(blocks):
+            out[to, index * T : (index + 1) * T, :] = part[:, at * 128 : (at + 1) * 128]
+        out[to, len(blocks) * T :, :] = tile
     store.wait()
 
 
@@ -402,7 +408,7 @@
     return pl.pallas_call(
         lambda *refs: search_kernel(first, last, *refs),
         out_shape=(
-            shape(N_ZH, T, 640 if last else BLOCK + 128, dtype=BF),
+            shape(N_ZH, (2 if last else 8) * T + 8, 128, dtype=BF),
             shape(T, 896 if last else WIDE),
         ),
         in_specs=[IN_VMEM, IN_SMEM, IN_VMEM, IN_VMEM] + [IN_HBM] * len(hbm),
@@ -412,11 +418,11 @@
     )(back, zh, weights, mat, *hbm)
 
 
-def middle_kernel(pieces, me, *refs):
-    cross, out = refs if len(refs) == 2 else (None, *refs)
-    tile = jnp.zeros((8, 128), F32)
+def middle_kernel(pieces, me, out):
+    total = jnp.zeros(pieces.shape[1:], F32)
     for source in range(N_MANY):
-        tile = tile + pieces[source].astype(F32)
+        total = total + pieces[source].astype(F32)
+    tile = total[-8:]
     high_a, low_a = split16(tile[0:1] + tile[1:2])
     high_b, low_b = split16(tile[2:3] + tile[3:4])
     line = lax.broadcasted_iota(jnp.int32, (8, 128), 0)
@@ -424,36 +430,32 @@
     for index, value in enumerate((high_a, low_a, high_b, low_b)):
         again = jnp.where(line == index, value, again)
     tile = jnp.where(me[0] == SCAL // 8, again, tile)
-    if cross is not None:
-        total = jnp.zeros((40, 128), F32)
-        for source in range(N_MANY):
-            total = total + cross[source].astype(F32)
-        tile = jnp.concatenate([total, tile], axis=0)
+    if total.shape[0] > 8:
+        tile = jnp.concatenate([total[:-8], tile], axis=0)
     tile = tile.astype(BF)
     for target in range(N_MANY):
         out[target] = tile
 
 
-def middle(pieces, me, cross=None):
-    extra = () if cross is None else (cross,)
+def middle(pieces, me):
     return pl.pallas_call(
         middle_kernel,
-        out_shape=shape(N_MANY, 48 if extra else 8, 128, dtype=BF),
-        in_specs=[IN_VMEM, IN_SMEM] + [IN_VMEM] * len(extra),
+        out_shape=shape(*pieces.shape, dtype=BF),
+        in_specs=[IN_VMEM, IN_SMEM],
         out_specs=IN_VMEM,
         compiler_params=PARAMS,
-    )(pieces, me, *extra)
+    )(pieces, me)
 
 
 def final_kernel(arrived, tail, penalty, answer_out, residual_out):
-    total = jnp.zeros((T, 640), F32)
+    total = jnp.zeros((2 * T + 8, 128), F32)
     for source in range(N_ZH):
         total = total + arrived[source].astype(F32)
-    square = total[:, 512:513] + total[:, 513:514]
+    square = from_tile(total[2 * T :])
     ridge = penalty[:, :1]
     mine = tail[:, :256]
     step = tail[:, 768:769] / (square + ridge * tail[:, 769:770])
-    hess = total[:, :256] + total[:, 256:512] + ridge * mine
+    hess = jnp.concatenate([total[:T], total[T : 2 * T]], axis=1) + ridge * mine
     answer_out[...] = tail[:, 256:512] + step * mine
     residual_out[...] = tail[:, 512:768] - step * hess
 
@@ -471,25 +473,22 @@
     fac = slots.reshape(BLOCK, RANK)
 
     spot = zh.reshape(1)
+    spot = zh.reshape(1)
     mat = exchange(pack(design, targets.T), OWN)
-    arrived = list(start(mat, spot))
-    for shift in range(1, N_ZH):
-        pairs = [(i, (i + shift) % N_ZH) for i in range(N_ZH)]
-        arrived[shift] = lax.ppermute(arrived[shift], "zh", pairs)
+    arrived = call(start_kernel, shape(N_ZH, T, BLOCK + 256, dtype=BF))(mat)
+    arrived = exchange(arrived, "zh")
     cross = call(cross_kernel, shape(N_MANY, 40, 128, dtype=BF))(mat, fac)
-    cross = exchange(cross, MANY)
 
     w = jnp.broadcast_to(weights[None, :], (8, RANK))
     ridge = jnp.broadcast_to(penalty[:, None], (T, 128))
 
-    packed, residual = first_call(arrived, mat, fac)
-    packed, cross = lax.optimization_barrier((packed, cross))
+    packed, residual = first_call(arrived, mat, fac, cross)
     fix = residual
     answer = state = full = None
     for step_index in range(ITERS):
         first, last = step_index == 0, step_index == ITERS - 1
-        pieces = exchange(packed.reshape(N_MANY, 8, 128), MANY)
-        back = exchange(middle(pieces, me, cross if first else None), MANY)
+        pieces = exchange(packed.reshape(N_MANY, -1, 128), MANY)
+        back = exchange(middle(pieces, me), MANY)
         if first:
             full = back
         else:

time: 233 us -> 228 us (0.979)
  starting transfers between devices: 45 us -> 41.1 us
    all_to_all x3, waiting for transfers between devices: 8.47 us -> 39.2 us  [exchange(): return lax.all_to_all(pieces, axes, 0, 0, tiled=True)]
    ppermute x3, waiting for transfers between devices: 29.1 us -> 9.31 us  [program(): other = lax.ppermute(low_factor, 'zh', pairs)]
    ppermute x3 -> x0, waiting for transfers between devices: 11.4 us -> none  [program(): arrived[shift] = lax.ppermute(arrived[shift], 'zh', pairs)]
    ppermute x3 -> x0, starting transfers between devices: 7.07 us -> none  [program(): arrived[shift] = lax.ppermute(arrived[shift], 'zh', pairs)]
    all_to_all x3, starting transfers between devices: 28.2 us -> 32.4 us  [exchange(): return lax.all_to_all(pieces, axes, 0, 0, tiled=True)]
    all_to_all x8, blocking collectives: 118 us -> 116 us  [exchange(): return lax.all_to_all(pieces, axes, 0, 0, tiled=True)]
  transfers between devices with their start and end apart: 9 -> 6, of which waited for: 5 -> 4; matrix products, arithmetic and copies ran while one was open for 0% -> 0% of each run, Pallas kernels for 1% -> 1%
where the time goes in v1:
time: 228 us; the launch traced here: 227 us
  blocking collectives  116 us (51%)
  waiting for transfers between devices  48.5 us (21%)
  starting transfers between devices  41.1 us (18%)
  Pallas kernels  18.8 us (8%)
    all_to_all x8, blocking collectives, exchange(): return lax.all_to_all(pieces, axes, 0, 0, tiled=True)  116 us
    all_to_all x3, waiting for transfers between devices, exchange(): return lax.all_to_all(pieces, axes, 0, 0, tiled=True)  39.2 us
    all_to_all x3, starting transfers between devices, exchange(): return lax.all_to_all(pieces, axes, 0, 0, tiled=True)  32.4 us
    ppermute x3, waiting for transfers between devices, program(): other = lax.ppermute(low_factor, 'zh', pairs)  9.31 us
    ppermute x3, starting transfers between devices, program(): other = lax.ppermute(low_factor, 'zh', pairs)  8.72 us
    pallas_call x3, Pallas kernels, search_call(): pl.pallas_call(lambda *refs: search_kernel(first, last, *refs), out_shape...  6.21 us
  transfers between devices with their start and end apart: 6, of which 4 were waited for; matrix products, arithmetic and copies ran while one was open for 0% of the time, Pallas kernels for 1%

profile of v1, /device:TPU:1, one launch (start us, length us, event | category | flops | bytes accessed | tf_op | source)
XLA Modules:
  0.0 226.8 jit_solution(10399264370968596037)
XLA Ops:
  0.6 3.2 %shard_map.68 = bf16[8,136,1024]{2,1,0:T(8,128)(2,1)} custom-call(bf16[128,8192]{1,0:T(8,128)(2,1)} %design.1, bf16[48,128]{1,0:T(8,128)(2,1)} %bitcast.29), custom_call_target="tpu_custom_call" | custom-call | tf_op jit(solution)/shard_map/pallas_call | solution.py:121
  3.9 0.0 copy-start.3
  3.9 6.5 %all-to-all-start = ((bf16[8,136,1024]{2,1,0:T(8,128)(2,1)}), bf16[8,136,1024]{2,1,0:T(8,128)(2,1)S(1)}, u32[]{:S(2)}, u32[]{:S(2)}) async-start(bf16[8,136,1024]{2,1,0:T(8,128)(2,1)} %shard_map.68), calls=%async_computation | async-start | bytes 4456448 | tf_op jit(solution)/shard_map/all_to_all | solution.py:24
  10.4 0.0 copy-done.3
  10.5 3.1 %collective-permute-start = (bf16[256,256]{1,0:T(8,128)(2,1)S(1)}, bf16[256,256]{1,0:T(8,128)(2,1)S(1)}, u32[]{:S(2)}, u32[]{:S(2)}) collective-permute-start(bf16[256,256]{1,0:T(8,128)(2,1)S(1)} %get-tuple-element.35), channel_id=1, source_target_pairs={{0,64},{64,128},{128,192},{192,0},{1,65},{65,129},{129,193},{193,1... | collective-permute-start | bytes 393224 | tf_op jit(solution)/shard_map/ppermute | solution.py:471
  13.6 24.5 %all-to-all-done.mat.refs_3_ = bf16[8,136,1024]{2,1,0:T(8,128)(2,1)S(1)} async-done(((bf16[8,136,1024]{2,1,0:T(8,128)(2,1)}), bf16[8,136,1024]{2,1,0:T(8,128)(2,1)S(1)}, u32[]{:S(2)}, u32[]{:S(2)}) %all-to-all-start) | async-done | bytes 2228256 | tf_op jit(solution)/shard_map/all_to_all | solution.py:24
  38.0 1.2 shard_map.69
  39.2 7.3 %all-to-all-start.1 = ((bf16[4,48,1280]{2,1,0:T(8,128)(2,1)}), bf16[4,48,1280]{2,1,0:T(8,128)(2,1)}, u32[]{:S(2)}, u32[]{:S(2)}) async-start(bf16[4,48,1280]{2,1,0:T(8,128)(2,1)} %shard_map.69), calls=%async_computation.1 | async-start | bytes 983040 | tf_op jit(solution)/shard_map/all_to_all | solution.py:24
  46.5 5.4 %collective-permute-start.1 = (bf16[256,256]{1,0:T(8,128)(2,1)S(1)}, bf16[256,256]{1,0:T(8,128)(2,1)S(1)}, u32[]{:S(2)}, u32[]{:S(2)}) collective-permute-start(bf16[256,256]{1,0:T(8,128)(2,1)S(1)} %get-tuple-element.35), channel_id=1, source_target_pairs={{0,128},{64,192},{128,0},{192,64},{1,129},{65,193},{129,1},{193,65... | collective-permute-start | bytes 393224 | tf_op jit(solution)/shard_map/ppermute | solution.py:471
  51.9 0.3 collective-permute-start.2
  52.2 0.0 collective-permute-done
  52.2 8.5 %collective-permute-done.1 = bf16[256,256]{1,0:T(8,128)(2,1)S(1)} collective-permute-done((bf16[256,256]{1,0:T(8,128)(2,1)S(1)}, bf16[256,256]{1,0:T(8,128)(2,1)S(1)}, u32[]{:S(2)}, u32[]{:S(2)}) %collective-permute-start.1) | collective-permute-done | bytes 131104 | tf_op jit(solution)/shard_map/ppermute | solution.py:471
  60.7 0.8 collective-permute-done.2
  61.5 0.9 shard_map.70.cross
  62.4 0.0 all-to-all-done.1.arrived
  62.4 2.3 %shard_map.71 = (bf16[64,48,128]{2,1,0:T(8,128)(2,1)S(1)}, f32[48,1280]{1,0:T(8,128)S(1)}) custom-call(bf16[4,48,1280]{2,1,0:T(8,128)(2,1)} %all-to-all-done.1.arrived, bf16[8,136,1024]{2,1,0:T(8,128)(2,1)S(1)} %all-to-all-done.mat.refs_3_, bf16[1024,256]{1,0:T(8,128)(2,1)S(1)} %bitcast.19, bf16[64,40,128]{2,1,0:T(8,128)(2,1)S(1)} %shard_map.70.cross), custom_call_target="tpu_custom_call" | custom-call | tf_op jit(solution)/shard_map/pallas_call | solution.py:202
  64.8 0.0 copy-start
  64.8 0.7 copy-done
  65.5 0.0 copy-start.2
  65.5 0.9 copy-done.2
  66.3 0.0 copy-start.4
  66.3 18.6 %all-to-all-start.2 = ((bf16[64,48,128]{2,1,0:T(8,128)(2,1)}), bf16[64,48,128]{2,1,0:T(8,128)(2,1)S(1)}, u32[]{:S(2)}, u32[]{:S(2)}) async-start(bf16[64,48,128]{2,1,0:T(8,128)(2,1)} %copy-done.2), calls=%async_computation.2 | async-start | bytes 1572864 | tf_op jit(solution)/shard_map/all_to_all | solution.py:24
  85.0 14.7 %all-to-all-done.2.pieces = bf16[64,48,128]{2,1,0:T(8,128)(2,1)S(1)} async-done(((bf16[64,48,128]{2,1,0:T(8,128)(2,1)}), bf16[64,48,128]{2,1,0:T(8,128)(2,1)S(1)}, u32[]{:S(2)}, u32[]{:S(2)}) %all-to-all-start.2) | async-done | bytes 786464 | tf_op jit(solution)/shard_map/all_to_all | solution.py:24
  99.7 0.0 copy-start.1
  99.7 0.2 shard_map.72
  99.9 19.4 %all_to_all.55.refs_0_.refs_7_ = bf16[64,48,128]{2,1,0:T(8,128)(2,1)S(1)} all-to-all(bf16[64,48,128]{2,1,0:T(8,128)(2,1)S(1)} %shard_map.72), channel_id=1, replica_groups=mesh['zh'=4,'zl'=2,'y'=4,'x'=4,'c'=2] {'zl','y','x','c'}, dimensions={0} | all-to-all | bytes 1572864 | tf_op jit(solution)/shard_map/all_to_all | solution.py:24
  119.3 0.0 copy-done.4
  119.3 0.0 copy-done.1
  119.3 0.0 copy-start.5
  119.3 1.7 shard_map.73
  121.0 16.7 %all_to_all.56.refs_0_ = bf16[4,392,128]{2,1,0:T(8,128)(2,1)S(1)} all-to-all(bf16[4,392,128]{2,1,0:T(8,128)(2,1)S(1)} %get-tuple-element.20), channel_id=1, replica_groups=mesh['zh'=4,'zl'=2,'y'=4,'x'=4,'c'=2] {'zh'}, dimensions={0} | all-to-all | bytes 802816 | tf_op jit(solution)/shard_map/all_to_all | solution.py:24
  137.8 0.0 copy-done.5
  137.8 0.1 broadcast_in_dim.33.refs_2_.penalty
  137.8 1.7 shard_map.74
  139.6 14.6 %all_to_all.57.pieces = bf16[64,8,128]{2,1,0:T(8,128)(2,1)S(1)} all-to-all(bf16[64,8,128]{2,1,0:T(8,128)(2,1)S(1)} %bitcast.28), channel_id=1, replica_groups=mesh['zh'=4,'zl'=2,'y'=4,'x'=4,'c'=2] {'zl','y','x','c'}, dimensions={0} | all-to-all | bytes 262144 | tf_op jit(solution)/shard_map/all_to_all | solution.py:24
  154.2 0.1 shard_map.75
  154.3 12.6 %all_to_all.58 = bf16[64,8,128]{2,1,0:T(8,128)(2,1)S(1)} all-to-all(bf16[64,8,128]{2,1,0:T(8,128)(2,1)S(1)} %shard_map.75), channel_id=1, replica_groups=mesh['zh'=4,'zl'=2,'y'=4,'x'=4,'c'=2] {'zl','y','x','c'}, dimensions={0} | all-to-all | bytes 262144 | tf_op jit(solution)/shard_map/all_to_all | solution.py:24
  166.9 2.2 shard_map.76
  169.2 15.1 %all_to_all.59.refs_0_ = bf16[4,392,128]{2,1,0:T(8,128)(2,1)S(1)} all-to-all(bf16[4,392,128]{2,1,0:T(8,128)(2,1)S(1)} %get-tuple-element.24), channel_id=1, replica_groups=mesh['zh'=4,'zl'=2,'y'=4,'x'=4,'c'=2] {'zh'}, dimensions={0} | all-to-all | bytes 802816 | tf_op jit(solution)/shard_map/all_to_all | solution.py:24
  184.2 2.0 shard_map.77
  186.2 15.2 %all_to_all.60.pieces = bf16[64,8,128]{2,1,0:T(8,128)(2,1)S(1)} all-to-all(bf16[64,8,128]{2,1,0:T(8,128)(2,1)S(1)} %bitcast.27), channel_id=1, replica_groups=mesh['zh'=4,'zl'=2,'y'=4,'x'=4,'c'=2] {'zl','y','x','c'}, dimensions={0} | all-to-all | bytes 262144 | tf_op jit(solution)/shard_map/all_to_all | solution.py:24
  201.5 0.1 shard_map.78
  201.5 12.6 %all_to_all.61 = bf16[64,8,128]{2,1,0:T(8,128)(2,1)S(1)} all-to-all(bf16[64,8,128]{2,1,0:T(8,128)(2,1)S(1)} %shard_map.78), channel_id=1, replica_groups=mesh['zh'=4,'zl'=2,'y'=4,'x'=4,'c'=2] {'zl','y','x','c'}, dimensions={0} | all-to-all | bytes 262144 | tf_op jit(solution)/shard_map/all_to_all | solution.py:24
  214.2 2.3 %shard_map.79 = (bf16[4,104,128]{2,1,0:T(8,128)(2,1)S(1)}, f32[48,896]{1,0:T(8,128)S(1)}) custom-call(bf16[512,128]{1,0:T(8,128)(2,1)S(1)} %bitcast.25, s32[1]{0:T(128)} %bitcast.7.refs_1_, f32[8,256]{1,0:T(8,128)S(1)} %broadcast_in_dim.32.refs_2_, bf16[8,136,1024]{2,1,0:T(8,128)(2,1)S(1)} %all-to-all-done.mat.refs_3_, ...), custom_call_target="tpu_custom_call" | custom-call | tf_op jit(solution)/shard_map/pallas_call | solution.py:408
  216.5 9.5 %all_to_all.62.arrived = bf16[4,104,128]{2,1,0:T(8,128)(2,1)S(1)} all-to-all(bf16[4,104,128]{2,1,0:T(8,128)(2,1)S(1)} %get-tuple-element.30), channel_id=1, replica_groups=mesh['zh'=4,'zl'=2,'y'=4,'x'=4,'c'=2] {'zh'}, dimensions={0} | all-to-all | bytes 212992 | tf_op jit(solution)/shard_map/all_to_all | solution.py:24
  226.0 0.9 shard_map.80
  (6 shorter events, 0.1 us)
Async XLA Ops:
  3.9 6.6 %copy-start.3 = (f32[256,256]{1,0:T(8,128)S(1)}, f32[256,256]{1,0:T(8,128)}, u32[]{:S(2)}) copy-start(f32[256,256]{1,0:T(8,128)} %param.7) | copy-start | bytes 786436
  3.9 34.1 %all-to-all-start = ((bf16[8,136,1024]{2,1,0:T(8,128)(2,1)}), bf16[8,136,1024]{2,1,0:T(8,128)(2,1)S(1)}, u32[]{:S(2)}, u32[]{:S(2)}) async-start(bf16[8,136,1024]{2,1,0:T(8,128)(2,1)} %shard_map.68), calls=%async_computation | async-start | bytes 4456448 | tf_op jit(solution)/shard_map/all_to_all | solution.py:24
  10.5 41.7 %collective-permute-start = (bf16[256,256]{1,0:T(8,128)(2,1)S(1)}, bf16[256,256]{1,0:T(8,128)(2,1)S(1)}, u32[]{:S(2)}, u32[]{:S(2)}) collective-permute-start(bf16[256,256]{1,0:T(8,128)(2,1)S(1)} %get-tuple-element.35), channel_id=1, source_target_pairs={{0,64},{64,128},{128,192},{192,0},{1,65},{65,129},{129,193},{193,1... | collective-permute-start | bytes 393224 | tf_op jit(solution)/shard_map/ppermute | solution.py:471
  39.2 23.2 %all-to-all-start.1 = ((bf16[4,48,1280]{2,1,0:T(8,128)(2,1)}), bf16[4,48,1280]{2,1,0:T(8,128)(2,1)}, u32[]{:S(2)}, u32[]{:S(2)}) async-start(bf16[4,48,1280]{2,1,0:T(8,128)(2,1)} %shard_map.69), calls=%async_computation.1 | async-start | bytes 983040 | tf_op jit(solution)/shard_map/all_to_all | solution.py:24
  46.5 14.2 %collective-permute-start.1 = (bf16[256,256]{1,0:T(8,128)(2,1)S(1)}, bf16[256,256]{1,0:T(8,128)(2,1)S(1)}, u32[]{:S(2)}, u32[]{:S(2)}) collective-permute-start(bf16[256,256]{1,0:T(8,128)(2,1)S(1)} %get-tuple-element.35), channel_id=1, source_target_pairs={{0,128},{64,192},{128,0},{192,64},{1,129},{65,193},{129,1},{193,65... | collective-permute-start | bytes 393224 | tf_op jit(solution)/shard_map/ppermute | solution.py:471
  51.9 9.6 %collective-permute-start.2 = (bf16[256,256]{1,0:T(8,128)(2,1)S(1)}, bf16[256,256]{1,0:T(8,128)(2,1)S(1)}, u32[]{:S(2)}, u32[]{:S(2)}) collective-permute-start(bf16[256,256]{1,0:T(8,128)(2,1)S(1)} %get-tuple-element.35), channel_id=1, source_target_pairs={{0,192},{64,0},{128,64},{192,128},{1,193},{65,1},{129,65},{193,129... | collective-permute-start | bytes 393224 | tf_op jit(solution)/shard_map/ppermute | solution.py:471
  64.8 0.7 copy-start
  65.5 0.9 copy-start.2
  66.3 53.0 %copy-start.4 = (f32[256]{0:T(256)S(1)}, f32[256]{0:T(256)}, u32[]{:S(2)}) copy-start(f32[256]{0:T(256)} %param.8) | copy-start | bytes 3076
  66.3 33.4 %all-to-all-start.2 = ((bf16[64,48,128]{2,1,0:T(8,128)(2,1)}), bf16[64,48,128]{2,1,0:T(8,128)(2,1)S(1)}, u32[]{:S(2)}, u32[]{:S(2)}) async-start(bf16[64,48,128]{2,1,0:T(8,128)(2,1)} %copy-done.2), calls=%async_computation.2 | async-start | bytes 1572864 | tf_op jit(solution)/shard_map/all_to_all | solution.py:24
  99.7 19.6 %copy-start.1 = (f32[48,1280]{1,0:T(8,128)S(1)}, f32[48,1280]{1,0:T(8,128)}, u32[]{:S(2)}) copy-start(f32[48,1280]{1,0:T(8,128)} %copy-done) | copy-start | bytes 737284
  119.3 18.5 %copy-start.5 = (f32[48]{0:T(128)S(1)}, f32[48]{0:T(128)}, u32[]{:S(2)}) copy-start(f32[48]{0:T(128)} %param.9) | copy-start | bytes 580

commit v2 on v1

--- a/solution.py
+++ b/solution.py
@@ -463,7 +463,11 @@
 def program(design, targets, factor, weights, penalty):
     zh = lax.axis_index("zh")
     me = lax.axis_index(MANY).reshape(1)
-    low_factor = factor.astype(BF)
+    w = jnp.broadcast_to(weights[None, :], (8, RANK))
+    ridge = jnp.broadcast_to(penalty[:, None], (T, 128))
+    low_factor, spot, me, w, ridge = lax.optimization_barrier(
+        (factor.astype(BF), zh.reshape(1), me, w, ridge)
+    )
     slots = jnp.zeros((N_ZH, 256, RANK), BF)
     slots = lax.dynamic_update_slice(slots, low_factor[None], (zh, 0, 0))
     for shift in range(1, N_ZH):
@@ -473,14 +477,10 @@
     fac = slots.reshape(BLOCK, RANK)
 
     spot = zh.reshape(1)
-    spot = zh.reshape(1)
     mat = exchange(pack(design, targets.T), OWN)
     arrived = call(start_kernel, shape(N_ZH, T, BLOCK + 256, dtype=BF))(mat)
     arrived = exchange(arrived, "zh")
     cross = call(cross_kernel, shape(N_MANY, 40, 128, dtype=BF))(mat, fac)
-
-    w = jnp.broadcast_to(weights[None, :], (8, RANK))
-    ridge = jnp.broadcast_to(penalty[:, None], (T, 128))
 
     packed, residual = first_call(arrived, mat, fac, cross)
     fix = residual

time: 228 us -> 216 us (0.947)
  blocking collectives: 116 us -> 140 us
  starting transfers between devices: 41.1 us -> 22.5 us
  waiting for transfers between devices: 48.5 us -> 33.2 us
    all_to_all x8 -> x9, blocking collectives: 116 us -> 140 us  [exchange(): return lax.all_to_all(pieces, axes, 0, 0, tiled=True)]
    all_to_all x3 -> x2, starting transfers between devices: 32.4 us -> 14.1 us  [exchange(): return lax.all_to_all(pieces, axes, 0, 0, tiled=True)]
    all_to_all x3 -> x2, waiting for transfers between devices: 39.2 us -> 30 us  [exchange(): return lax.all_to_all(pieces, axes, 0, 0, tiled=True)]
    ppermute x3, waiting for transfers between devices: 9.31 us -> 3.18 us  [program(): other = lax.ppermute(low_factor, 'zh', pairs)]
  transfers between devices with their start and end apart: 6 -> 5, of which waited for: 4 -> 3; matrix products, arithmetic and copies ran while one was open for 0% -> 0% of each run, Pallas kernels for 1% -> 1%
where the time goes in v2:
time: 216 us; the launch traced here: 215 us
  blocking collectives  140 us (65%)
  waiting for transfers between devices  33.2 us (15%)
  starting transfers between devices  22.5 us (10%)
  Pallas kernels  18.8 us (9%)
    all_to_all x9, blocking collectives, exchange(): return lax.all_to_all(pieces, axes, 0, 0, tiled=True)  140 us
    all_to_all x2, waiting for transfers between devices, exchange(): return lax.all_to_all(pieces, axes, 0, 0, tiled=True)  30 us
    all_to_all x2, starting transfers between devices, exchange(): return lax.all_to_all(pieces, axes, 0, 0, tiled=True)  14.1 us
    ppermute x3, starting transfers between devices, program(): other = lax.ppermute(low_factor, 'zh', pairs)  8.4 us
    pallas_call x3, Pallas kernels, search_call(): pl.pallas_call(lambda *refs: search_kernel(first, last, *refs), out_shape...  6.2 us
  transfers between devices with their start and end apart: 5, of which 3 were waited for; matrix products, arithmetic and copies ran while one was open for 0% of the time, Pallas kernels for 1%

profile of v2, /device:TPU:1, one launch (start us, length us, event | category | flops | bytes accessed | tf_op | source)
XLA Modules:
  0.0 215.2 jit_solution(11369114874197927855)
XLA Ops:
  0.6 3.2 %shard_map.68 = bf16[8,136,1024]{2,1,0:T(8,128)(2,1)} custom-call(bf16[128,8192]{1,0:T(8,128)(2,1)} %design.1, bf16[48,128]{1,0:T(8,128)(2,1)} %bitcast.29), custom_call_target="tpu_custom_call" | custom-call | tf_op jit(solution)/shard_map/pallas_call | solution.py:121
  3.9 0.0 copy-start
  3.9 0.0 copy-start.1
  3.9 0.0 copy-start.2
  3.9 6.5 %all-to-all-start = ((bf16[8,136,1024]{2,1,0:T(8,128)(2,1)}), bf16[8,136,1024]{2,1,0:T(8,128)(2,1)S(1)}, u32[]{:S(2)}, u32[]{:S(2)}) async-start(bf16[8,136,1024]{2,1,0:T(8,128)(2,1)} %shard_map.68), calls=%async_computation | async-start | bytes 4456448 | tf_op jit(solution)/shard_map/all_to_all | solution.py:24
  10.4 0.0 copy-done
  10.5 0.0 copy-done.1
  10.5 0.0 copy-done.2
  10.5 0.1 broadcast_in_dim.29.refs_2_.penalty
  10.6 5.1 %collective-permute-start.2 = (bf16[256,256]{1,0:T(8,128)(2,1)S(1)}, bf16[256,256]{1,0:T(8,128)(2,1)S(1)}, u32[]{:S(2)}, u32[]{:S(2)}) collective-permute-start(bf16[256,256]{1,0:T(8,128)(2,1)S(1)} %convert_element_type.3), channel_id=1, source_target_pairs={{0,192},{64,0},{128,64},{192,128},{1,193},{65,1},{129,65},{193,129... | collective-permute-start | bytes 393224 | tf_op jit(solution)/shard_map/ppermute | solution.py:475
  15.7 1.2 collective-permute-start.1
  16.9 2.1 collective-permute-start
  19.0 19.8 %all-to-all-done.mat.refs_3_ = bf16[8,136,1024]{2,1,0:T(8,128)(2,1)S(1)} async-done(((bf16[8,136,1024]{2,1,0:T(8,128)(2,1)}), bf16[8,136,1024]{2,1,0:T(8,128)(2,1)S(1)}, u32[]{:S(2)}, u32[]{:S(2)}) %all-to-all-start) | async-done | bytes 2228256 | tf_op jit(solution)/shard_map/all_to_all | solution.py:24
  38.8 1.2 shard_map.69
  40.0 7.6 %all-to-all-start.1 = ((bf16[4,48,1280]{2,1,0:T(8,128)(2,1)}), bf16[4,48,1280]{2,1,0:T(8,128)(2,1)}, u32[]{:S(2)}, u32[]{:S(2)}) async-start(bf16[4,48,1280]{2,1,0:T(8,128)(2,1)} %shard_map.69), calls=%async_computation.1 | async-start | bytes 983040 | tf_op jit(solution)/shard_map/all_to_all | solution.py:24
  47.7 3.2 %collective-permute-done = bf16[256,256]{1,0:T(8,128)(2,1)S(1)} collective-permute-done((bf16[256,256]{1,0:T(8,128)(2,1)S(1)}, bf16[256,256]{1,0:T(8,128)(2,1)S(1)}, u32[]{:S(2)}, u32[]{:S(2)}) %collective-permute-start) | collective-permute-done | bytes 131104 | tf_op jit(solution)/shard_map/ppermute | solution.py:475
  50.9 0.0 collective-permute-done.1
  51.0 0.0 collective-permute-done.2
  51.0 0.9 shard_map.70.cross
  51.9 10.2 %all-to-all-done.1.arrived = bf16[4,48,1280]{2,1,0:T(8,128)(2,1)} async-done(((bf16[4,48,1280]{2,1,0:T(8,128)(2,1)}), bf16[4,48,1280]{2,1,0:T(8,128)(2,1)}, u32[]{:S(2)}, u32[]{:S(2)}) %all-to-all-start.1) | async-done | bytes 491552 | tf_op jit(solution)/shard_map/all_to_all | solution.py:24
  62.1 2.3 %shard_map.71 = (bf16[64,48,128]{2,1,0:T(8,128)(2,1)S(1)}, f32[48,1280]{1,0:T(8,128)S(1)}) custom-call(bf16[4,48,1280]{2,1,0:T(8,128)(2,1)} %all-to-all-done.1.arrived, bf16[8,136,1024]{2,1,0:T(8,128)(2,1)S(1)} %all-to-all-done.mat.refs_3_, bf16[1024,256]{1,0:T(8,128)(2,1)S(1)} %bitcast.19, bf16[64,40,128]{2,1,0:T(8,128)(2,1)S(1)} %shard_map.70.cross), custom_call_target="tpu_custom_call" | custom-call | tf_op jit(solution)/shard_map/pallas_call | solution.py:202
  64.4 24.6 %all_to_all.55.pieces = bf16[64,48,128]{2,1,0:T(8,128)(2,1)S(1)} all-to-all(bf16[64,48,128]{2,1,0:T(8,128)(2,1)S(1)} %get-tuple-element.23), channel_id=1, replica_groups=mesh['zh'=4,'zl'=2,'y'=4,'x'=4,'c'=2] {'zl','y','x','c'}, dimensions={0} | all-to-all | bytes 1572864 | tf_op jit(solution)/shard_map/all_to_all | solution.py:24
  89.0 0.2 shard_map.72
  89.1 19.4 %all_to_all.56.refs_0_.refs_7_ = bf16[64,48,128]{2,1,0:T(8,128)(2,1)S(1)} all-to-all(bf16[64,48,128]{2,1,0:T(8,128)(2,1)S(1)} %shard_map.72), channel_id=1, replica_groups=mesh['zh'=4,'zl'=2,'y'=4,'x'=4,'c'=2] {'zl','y','x','c'}, dimensions={0} | all-to-all | bytes 1572864 | tf_op jit(solution)/shard_map/all_to_all | solution.py:24
  108.6 1.7 shard_map.73
  110.3 16.0 %all_to_all.57.refs_0_ = bf16[4,392,128]{2,1,0:T(8,128)(2,1)S(1)} all-to-all(bf16[4,392,128]{2,1,0:T(8,128)(2,1)S(1)} %get-tuple-element.27), channel_id=1, replica_groups=mesh['zh'=4,'zl'=2,'y'=4,'x'=4,'c'=2] {'zh'}, dimensions={0} | all-to-all | bytes 802816 | tf_op jit(solution)/shard_map/all_to_all | solution.py:24
  126.2 1.7 shard_map.74
  128.0 14.6 %all_to_all.58.pieces = bf16[64,8,128]{2,1,0:T(8,128)(2,1)S(1)} all-to-all(bf16[64,8,128]{2,1,0:T(8,128)(2,1)S(1)} %bitcast.28), channel_id=1, replica_groups=mesh['zh'=4,'zl'=2,'y'=4,'x'=4,'c'=2] {'zl','y','x','c'}, dimensions={0} | all-to-all | bytes 262144 | tf_op jit(solution)/shard_map/all_to_all | solution.py:24
  142.6 0.1 shard_map.75
  142.7 12.6 %all_to_all.59 = bf16[64,8,128]{2,1,0:T(8,128)(2,1)S(1)} all-to-all(bf16[64,8,128]{2,1,0:T(8,128)(2,1)S(1)} %shard_map.75), channel_id=1, replica_groups=mesh['zh'=4,'zl'=2,'y'=4,'x'=4,'c'=2] {'zl','y','x','c'}, dimensions={0} | all-to-all | bytes 262144 | tf_op jit(solution)/shard_map/all_to_all | solution.py:24
  155.3 2.2 %shard_map.76 = (bf16[4,392,128]{2,1,0:T(8,128)(2,1)S(1)}, f32[48,2432]{1,0:T(8,128)S(1)}) custom-call(bf16[512,128]{1,0:T(8,128)(2,1)S(1)} %bitcast.26, s32[1]{0:T(128)} %bitcast.1.refs_1_, f32[8,256]{1,0:T(8,128)S(1)} %broadcast_in_dim.28.refs_2_, bf16[8,136,1024]{2,1,0:T(8,128)(2,1)S(1)} %all-to-all-done.mat.refs_3_, ...), custom_call_target="tpu_custom_call" | custom-call | tf_op jit(solution)/shard_map/pallas_call | solution.py:408
  157.6 15.1 %all_to_all.60.refs_0_ = bf16[4,392,128]{2,1,0:T(8,128)(2,1)S(1)} all-to-all(bf16[4,392,128]{2,1,0:T(8,128)(2,1)S(1)} %get-tuple-element.32), channel_id=1, replica_groups=mesh['zh'=4,'zl'=2,'y'=4,'x'=4,'c'=2] {'zh'}, dimensions={0} | all-to-all | bytes 802816 | tf_op jit(solution)/shard_map/all_to_all | solution.py:24
  172.6 2.0 shard_map.77
  174.6 15.2 %all_to_all.61.pieces = bf16[64,8,128]{2,1,0:T(8,128)(2,1)S(1)} all-to-all(bf16[64,8,128]{2,1,0:T(8,128)(2,1)S(1)} %bitcast.27), channel_id=1, replica_groups=mesh['zh'=4,'zl'=2,'y'=4,'x'=4,'c'=2] {'zl','y','x','c'}, dimensions={0} | all-to-all | bytes 262144 | tf_op jit(solution)/shard_map/all_to_all | solution.py:24
  189.9 0.1 shard_map.78
  189.9 12.6 %all_to_all.62 = bf16[64,8,128]{2,1,0:T(8,128)(2,1)S(1)} all-to-all(bf16[64,8,128]{2,1,0:T(8,128)(2,1)S(1)} %shard_map.78), channel_id=1, replica_groups=mesh['zh'=4,'zl'=2,'y'=4,'x'=4,'c'=2] {'zl','y','x','c'}, dimensions={0} | all-to-all | bytes 262144 | tf_op jit(solution)/shard_map/all_to_all | solution.py:24
  202.6 2.3 %shard_map.79 = (bf16[4,104,128]{2,1,0:T(8,128)(2,1)S(1)}, f32[48,896]{1,0:T(8,128)S(1)}) custom-call(bf16[512,128]{1,0:T(8,128)(2,1)S(1)} %bitcast.25, s32[1]{0:T(128)} %bitcast.1.refs_1_, f32[8,256]{1,0:T(8,128)S(1)} %broadcast_in_dim.28.refs_2_, bf16[8,136,1024]{2,1,0:T(8,128)(2,1)S(1)} %all-to-all-done.mat.refs_3_, ...), custom_call_target="tpu_custom_call" | custom-call | tf_op jit(solution)/shard_map/pallas_call | solution.py:408
  204.9 9.5 %all_to_all.63.arrived = bf16[4,104,128]{2,1,0:T(8,128)(2,1)S(1)} all-to-all(bf16[4,104,128]{2,1,0:T(8,128)(2,1)S(1)} %get-tuple-element.38), channel_id=1, replica_groups=mesh['zh'=4,'zl'=2,'y'=4,'x'=4,'c'=2] {'zh'}, dimensions={0} | all-to-all | bytes 212992 | tf_op jit(solution)/shard_map/all_to_all | solution.py:24
  214.4 0.9 shard_map.80
  (7 shorter events, 0.1 us)
Async XLA Ops:
  3.9 6.5 %copy-start = (f32[256,256]{1,0:T(8,128)S(1)}, f32[256,256]{1,0:T(8,128)}, u32[]{:S(2)}) copy-start(f32[256,256]{1,0:T(8,128)} %param.7) | copy-start | bytes 786436
  3.9 6.6 %copy-start.1 = (f32[256]{0:T(256)S(1)}, f32[256]{0:T(256)}, u32[]{:S(2)}) copy-start(f32[256]{0:T(256)} %param.8) | copy-start | bytes 3076
  3.9 6.6 %copy-start.2 = (f32[48]{0:T(128)S(1)}, f32[48]{0:T(128)}, u32[]{:S(2)}) copy-start(f32[48]{0:T(128)} %param.9) | copy-start | bytes 580
  3.9 34.9 %all-to-all-start = ((bf16[8,136,1024]{2,1,0:T(8,128)(2,1)}), bf16[8,136,1024]{2,1,0:T(8,128)(2,1)S(1)}, u32[]{:S(2)}, u32[]{:S(2)}) async-start(bf16[8,136,1024]{2,1,0:T(8,128)(2,1)} %shard_map.68), calls=%async_computation | async-start | bytes 4456448 | tf_op jit(solution)/shard_map/all_to_all | solution.py:24
  10.6 40.4 %collective-permute-start.2 = (bf16[256,256]{1,0:T(8,128)(2,1)S(1)}, bf16[256,256]{1,0:T(8,128)(2,1)S(1)}, u32[]{:S(2)}, u32[]{:S(2)}) collective-permute-start(bf16[256,256]{1,0:T(8,128)(2,1)S(1)} %convert_element_type.3), channel_id=1, source_target_pairs={{0,192},{64,0},{128,64},{192,128},{1,193},{65,1},{129,65},{193,129... | collective-permute-start | bytes 393224 | tf_op jit(solution)/shard_map/ppermute | solution.py:475
  15.7 35.2 %collective-permute-start.1 = (bf16[256,256]{1,0:T(8,128)(2,1)S(1)}, bf16[256,256]{1,0:T(8,128)(2,1)S(1)}, u32[]{:S(2)}, u32[]{:S(2)}) collective-permute-start(bf16[256,256]{1,0:T(8,128)(2,1)S(1)} %convert_element_type.3), channel_id=1, source_target_pairs={{0,128},{64,192},{128,0},{192,64},{1,129},{65,193},{129,1},{193,65... | collective-permute-start | bytes 393224 | tf_op jit(solution)/shard_map/ppermute | solution.py:475
  16.9 34.1 %collective-permute-start = (bf16[256,256]{1,0:T(8,128)(2,1)S(1)}, bf16[256,256]{1,0:T(8,128)(2,1)S(1)}, u32[]{:S(2)}, u32[]{:S(2)}) collective-permute-start(bf16[256,256]{1,0:T(8,128)(2,1)S(1)} %convert_element_type.3), channel_id=1, source_target_pairs={{0,64},{64,128},{128,192},{192,0},{1,65},{65,129},{129,193},{193,1... | collective-permute-start | bytes 393224 | tf_op jit(solution)/shard_map/ppermute | solution.py:475
  40.0 22.1 %all-to-all-start.1 = ((bf16[4,48,1280]{2,1,0:T(8,128)(2,1)}), bf16[4,48,1280]{2,1,0:T(8,128)(2,1)}, u32[]{:S(2)}, u32[]{:S(2)}) async-start(bf16[4,48,1280]{2,1,0:T(8,128)(2,1)} %shard_map.69), calls=%async_computation.1 | async-start | bytes 983040 | tf_op jit(solution)/shard_map/all_to_all | solution.py:24

commit v3 on v2

--- a/solution.py
+++ b/solution.py
@@ -12,7 +12,7 @@
 FEAT = ("x", "c")
 OWN = ("zl", "y")
 MANY = ("zl", "y", "x", "c")
-N_MANY, N_ZH = 64, 4
+N_OWN, N_MANY, N_ZH = 8, 64, 4
 T, RANK, BLOCK = 48, 256, 1024
 SCAL = 480
 HEAD = 512
@@ -85,7 +85,7 @@
 CHUNKS, DEEP = 4, 32
 
 
-def pack_kernel(design, goal, out, rows, packed, goals, sems):
+def pack_kernel(design, out, rows, packed, sems):
     def inward(index):
         at = pl.ds(index * DEEP, DEEP)
         return pltpu.make_async_copy(design.at[at, :], rows.at[at, :], sems.at[index])
@@ -98,12 +98,6 @@
 
     for index in range(CHUNKS):
         inward(index).start()
-    for to in range(8):
-        for index in range(6):
-            goals[to, :, index * 128 : (index + 1) * 128] = goal[index * 8 : index * 8 + 8, :]
-        goals[to, :, 768:] = jnp.zeros((8, 256), BF)
-    last = pltpu.make_async_copy(goals, out.at[:, 128:136, :], sems.at[2 * CHUNKS])
-    last.start()
     for index in range(CHUNKS):
         inward(index).wait()
         low, high = index * DEEP, (index + 1) * DEEP
@@ -114,36 +108,42 @@
         outward(index).start()
     for index in range(CHUNKS):
         outward(index).wait()
-    last.wait()
-
-
-def pack(design, goal):
+
+
+def pack(design):
     return pl.pallas_call(
         pack_kernel,
-        out_shape=shape(8, 136, BLOCK, dtype=BF),
-        in_specs=[IN_HBM, IN_VMEM],
+        out_shape=shape(8, 128, BLOCK, dtype=BF),
+        in_specs=[IN_HBM],
         out_specs=IN_HBM,
         scratch_shapes=[
             pltpu.VMEM((128, 8192), BF),
             pltpu.VMEM((8, 128, BLOCK), BF),
-            pltpu.VMEM((8, 8, BLOCK), BF),
-            pltpu.SemaphoreType.DMA((2 * CHUNKS + 1,)),
+            pltpu.SemaphoreType.DMA((2 * CHUNKS,)),
         ],
-    )(design, goal)
-
-
-def start_kernel(mat, out):
+    )(design)
+
+
+def start_kernel(mat, owner, *refs):
+    goals, out = refs[:-1], refs[-1]
     part = jnp.zeros((T, BLOCK), F32)
-    for src in range(8):
-        goal = jnp.concatenate(
-            [mat[src, 128:136, t * 128 : (t + 1) * 128].astype(F32) for t in range(6)], axis=0
-        ).astype(BF)
-        part = part + dot(goal, mat[src, :128, :])
+    for shift, goal in enumerate(goals):
+        part = part + dot(goal[...], mat[lax.rem(owner[0] - shift + N_OWN, N_OWN)])
     high, low = split16(part)
     high, low = high.astype(BF), low.astype(BF)
     for to in range(N_ZH):
         out[to, :, :BLOCK] = high
         out[to, :, BLOCK:] = low[:, to * 256 : (to + 1) * 256]
+
+
+def start(mat, owner, goals):
+    return pl.pallas_call(
+        start_kernel,
+        out_shape=shape(N_ZH, T, BLOCK + 256, dtype=BF),
+        in_specs=[IN_VMEM, IN_SMEM] + [IN_VMEM] * len(goals),
+        out_specs=IN_VMEM,
+        compiler_params=PARAMS,
+    )(mat, owner, *goals)
 
 
 def cross_kernel(mat, fac, out):
@@ -465,8 +465,9 @@
     me = lax.axis_index(MANY).reshape(1)
     w = jnp.broadcast_to(weights[None, :], (8, RANK))
     ridge = jnp.broadcast_to(penalty[:, None], (T, 128))
-    low_factor, spot, me, w, ridge = lax.optimization_barrier(
-        (factor.astype(BF), zh.reshape(1), me, w, ridge)
+    owner = lax.axis_index(OWN).reshape(1)
+    low_factor, spot, owner, me, w, ridge = lax.optimization_barrier(
+        (factor.astype(BF), zh.reshape(1), owner, me, w, ridge)
     )
     slots = jnp.zeros((N_ZH, 256, RANK), BF)
     slots = lax.dynamic_update_slice(slots, low_factor[None], (zh, 0, 0))
@@ -477,8 +478,12 @@
     fac = slots.reshape(BLOCK, RANK)
 
     spot = zh.reshape(1)
-    mat = exchange(pack(design, targets.T), OWN)
-    arrived = call(start_kernel, shape(N_ZH, T, BLOCK + 256, dtype=BF))(mat)
+    goals = [targets.T]
+    for shift in range(1, N_OWN):
+        pairs = [(i, (i + shift) % N_OWN) for i in range(N_OWN)]
+        goals.append(lax.ppermute(goals[0], OWN, pairs))
+    mat = exchange(pack(design), OWN)
+    arrived = start(mat, owner, goals)
     arrived = exchange(arrived, "zh")
     cross = call(cross_kernel, shape(N_MANY, 40, 128, dtype=BF))(mat, fac)
 

time: 216 us -> 223 us (1.032)
  starting transfers between devices: 22.5 us -> 28.8 us
  blocking collectives: 140 us -> 146 us
  waiting for transfers between devices: 33.2 us -> 28.7 us
    all_to_all x2, waiting for transfers between devices: 30 us -> 9.52 us  [exchange(): return lax.all_to_all(pieces, axes, 0, 0, tiled=True)]
    ppermute x0 -> x7, waiting for transfers between devices: none -> 17.5 us  [program(): goals.append(lax.ppermute(goals[0], OWN, pairs))]
    ppermute x0 -> x7, starting transfers between devices: none -> 9.8 us  [program(): goals.append(lax.ppermute(goals[0], OWN, pairs))]
    all_to_all x9, blocking collectives: 140 us -> 146 us  [exchange(): return lax.all_to_all(pieces, axes, 0, 0, tiled=True)]
    all_to_all x2, starting transfers between devices: 14.1 us -> 10.6 us  [exchange(): return lax.all_to_all(pieces, axes, 0, 0, tiled=True)]
  transfers between devices with their start and end apart: 5 -> 12, of which waited for: 3 -> 3; matrix products, arithmetic and copies ran while one was open for 0% -> 0% of each run, Pallas kernels for 1% -> 1%
where the time goes in v3:
time: 223 us
  blocking collectives  146 us (65%)
  starting transfers between devices  28.8 us (13%)
  waiting for transfers between devices  28.7 us (13%)
  Pallas kernels  18 us (8%)
    all_to_all x9, blocking collectives, exchange(): return lax.all_to_all(pieces, axes, 0, 0, tiled=True)  146 us
    ppermute x7, waiting for transfers between devices, program(): goals.append(lax.ppermute(goals[0], OWN, pairs))  17.5 us
    all_to_all x2, starting transfers between devices, exchange(): return lax.all_to_all(pieces, axes, 0, 0, tiled=True)  10.6 us
    ppermute x7, starting transfers between devices, program(): goals.append(lax.ppermute(goals[0], OWN, pairs))  9.8 us
    all_to_all x2, waiting for transfers between devices, exchange(): return lax.all_to_all(pieces, axes, 0, 0, tiled=True)  9.52 us
    ppermute x3, starting transfers between devices, program(): other = lax.ppermute(low_factor, 'zh', pairs)  8.4 us
    pallas_call x3, Pallas kernels, search_call(): pl.pallas_call(lambda *refs: search_kernel(first, last, *refs), out_shape...  6.2 us
  transfers between devices with their start and end apart: 12, of which 3 were waited for; matrix products, arithmetic and copies ran while one was open for 0% of the time, Pallas kernels for 1%

profile of v3, /device:TPU:1, one launch (start us, length us, event | category | flops | bytes accessed | tf_op | source)
XLA Modules:
  0.0 222.7 jit_solution(4053040853767083621)
XLA Ops:
  0.6 2.5 %shard_map.68 = bf16[8,128,1024]{2,1,0:T(8,128)(2,1)} custom-call(bf16[128,8192]{1,0:T(8,128)(2,1)} %design.1), custom_call_target="tpu_custom_call" | custom-call | tf_op jit(solution)/shard_map/pallas_call | solution.py:114
  3.1 0.0 copy-start
  3.1 0.0 copy-start.1
  3.1 0.0 copy-start.2
  3.1 0.0 copy-start.3
  3.2 6.5 %all-to-all-start = ((bf16[8,128,1024]{2,1,0:T(8,128)(2,1)}), bf16[8,128,1024]{2,1,0:T(8,128)(2,1)S(1)}, u32[]{:S(2)}, u32[]{:S(2)}) async-start(bf16[8,128,1024]{2,1,0:T(8,128)(2,1)} %shard_map.68), calls=%async_computation | async-start | bytes 4194304 | tf_op jit(solution)/shard_map/all_to_all | solution.py:24
  9.7 3.6 %collective-permute-start.6 = (bf16[48,128]{1,0:T(8,128)(2,1)S(1)}, bf16[48,128]{1,0:T(8,128)(2,1)S(1)}, u32[]{:S(2)}, u32[]{:S(2)}) collective-permute-start(bf16[48,128]{1,0:T(8,128)(2,1)S(1)} %bitcast.30), channel_id=1, source_target_pairs={{0,56},{8,0},{16,8},{24,16},{32,24},{40,32},{48,40},{56,48},{1,57}... | collective-permute-start | bytes 36872 | tf_op jit(solution)/shard_map/ppermute | solution.py:484
  13.2 0.6 collective-permute-start.5
  13.8 0.6 collective-permute-start.4
  14.4 1.2 collective-permute-start.3
  15.6 1.2 collective-permute-start.2
  16.8 17.5 %collective-permute-done.6.refs_7_ = bf16[48,128]{1,0:T(8,128)(2,1)S(1)} collective-permute-done((bf16[48,128]{1,0:T(8,128)(2,1)S(1)}, bf16[48,128]{1,0:T(8,128)(2,1)S(1)}, u32[]{:S(2)}, u32[]{:S(2)}) %collective-permute-start.6) | collective-permute-done | bytes 12320 | tf_op jit(solution)/shard_map/ppermute | solution.py:484
  34.3 2.4 %collective-permute-start.1 = (bf16[48,128]{1,0:T(8,128)(2,1)S(1)}, bf16[48,128]{1,0:T(8,128)(2,1)S(1)}, u32[]{:S(2)}, u32[]{:S(2)}) collective-permute-start(bf16[48,128]{1,0:T(8,128)(2,1)S(1)} %bitcast.35), channel_id=1, source_target_pairs={{0,16},{8,24},{16,32},{24,40},{32,48},{40,56},{48,0},{56,8},{1,17}... | collective-permute-start | bytes 36872 | tf_op jit(solution)/shard_map/ppermute | solution.py:484
  36.7 0.0 collective-permute-done.5.refs_6_
  36.7 0.3 collective-permute-start
  37.1 0.1 broadcast_in_dim.28.refs_2_.penalty
  37.1 0.0 collective-permute-done.4.refs_5_
  37.1 5.1 %collective-permute-start.9 = (bf16[256,256]{1,0:T(8,128)(2,1)S(1)}, bf16[256,256]{1,0:T(8,128)(2,1)S(1)}, u32[]{:S(2)}, u32[]{:S(2)}) collective-permute-start(bf16[256,256]{1,0:T(8,128)(2,1)S(1)} %convert_element_type.3), channel_id=1, source_target_pairs={{0,192},{64,0},{128,64},{192,128},{1,193},{65,1},{129,65},{193,129... | collective-permute-start | bytes 393224 | tf_op jit(solution)/shard_map/ppermute | solution.py:476
  42.3 0.0 collective-permute-done.3.refs_4_
  42.3 1.2 collective-permute-start.8
  43.5 0.0 collective-permute-done.2.refs_3_
  43.5 2.1 collective-permute-start.7
  45.6 0.0 collective-permute-done.refs_1_
  45.6 0.0 all-to-all-done.mat.refs_3_
  45.6 1.2 shard_map.69
  46.8 4.1 %all-to-all-start.1 = ((bf16[4,48,1280]{2,1,0:T(8,128)(2,1)}), bf16[4,48,1280]{2,1,0:T(8,128)(2,1)}, u32[]{:S(2)}, u32[]{:S(2)}) async-start(bf16[4,48,1280]{2,1,0:T(8,128)(2,1)} %shard_map.69), calls=%async_computation.1 | async-start | bytes 983040 | tf_op jit(solution)/shard_map/all_to_all | solution.py:24
  51.1 1.6 collective-permute-done.7
  52.8 0.9 shard_map.70.cross
  53.6 9.5 %all-to-all-done.1.arrived = bf16[4,48,1280]{2,1,0:T(8,128)(2,1)} async-done(((bf16[4,48,1280]{2,1,0:T(8,128)(2,1)}), bf16[4,48,1280]{2,1,0:T(8,128)(2,1)}, u32[]{:S(2)}, u32[]{:S(2)}) %all-to-all-start.1) | async-done | bytes 491552 | tf_op jit(solution)/shard_map/all_to_all | solution.py:24
  63.2 2.3 %shard_map.71 = (bf16[64,48,128]{2,1,0:T(8,128)(2,1)S(1)}, f32[48,1280]{1,0:T(8,128)S(1)}) custom-call(bf16[4,48,1280]{2,1,0:T(8,128)(2,1)} %all-to-all-done.1.arrived, bf16[8,128,1024]{2,1,0:T(8,128)(2,1)S(1)} %all-to-all-done.mat.refs_3_, bf16[1024,256]{1,0:T(8,128)(2,1)S(1)} %bitcast.20, bf16[64,40,128]{2,1,0:T(8,128)(2,1)S(1)} %shard_map.70.cross), custom_call_target="tpu_custom_call" | custom-call | tf_op jit(solution)/shard_map/pallas_call | solution.py:202
  65.5 31.1 %all_to_all.55.pieces = bf16[64,48,128]{2,1,0:T(8,128)(2,1)S(1)} all-to-all(bf16[64,48,128]{2,1,0:T(8,128)(2,1)S(1)} %get-tuple-element.25), channel_id=1, replica_groups=mesh['zh'=4,'zl'=2,'y'=4,'x'=4,'c'=2] {'zl','y','x','c'}, dimensions={0} | all-to-all | bytes 1572864 | tf_op jit(solution)/shard_map/all_to_all | solution.py:24
  96.6 0.2 shard_map.72
  96.8 19.4 %all_to_all.56.refs_0_.refs_7_ = bf16[64,48,128]{2,1,0:T(8,128)(2,1)S(1)} all-to-all(bf16[64,48,128]{2,1,0:T(8,128)(2,1)S(1)} %shard_map.72), channel_id=1, replica_groups=mesh['zh'=4,'zl'=2,'y'=4,'x'=4,'c'=2] {'zl','y','x','c'}, dimensions={0} | all-to-all | bytes 1572864 | tf_op jit(solution)/shard_map/all_to_all | solution.py:24
  116.2 1.7 shard_map.73
  117.9 15.9 %all_to_all.57.refs_0_ = bf16[4,392,128]{2,1,0:T(8,128)(2,1)S(1)} all-to-all(bf16[4,392,128]{2,1,0:T(8,128)(2,1)S(1)} %get-tuple-element.29), channel_id=1, replica_groups=mesh['zh'=4,'zl'=2,'y'=4,'x'=4,'c'=2] {'zh'}, dimensions={0} | all-to-all | bytes 802816 | tf_op jit(solution)/shard_map/all_to_all | solution.py:24
  133.9 1.7 shard_map.74
  135.6 14.6 %all_to_all.58.pieces = bf16[64,8,128]{2,1,0:T(8,128)(2,1)S(1)} all-to-all(bf16[64,8,128]{2,1,0:T(8,128)(2,1)S(1)} %bitcast.29), channel_id=1, replica_groups=mesh['zh'=4,'zl'=2,'y'=4,'x'=4,'c'=2] {'zl','y','x','c'}, dimensions={0} | all-to-all | bytes 262144 | tf_op jit(solution)/shard_map/all_to_all | solution.py:24
  150.2 0.1 shard_map.75
  150.3 12.6 %all_to_all.59 = bf16[64,8,128]{2,1,0:T(8,128)(2,1)S(1)} all-to-all(bf16[64,8,128]{2,1,0:T(8,128)(2,1)S(1)} %shard_map.75), channel_id=1, replica_groups=mesh['zh'=4,'zl'=2,'y'=4,'x'=4,'c'=2] {'zl','y','x','c'}, dimensions={0} | all-to-all | bytes 262144 | tf_op jit(solution)/shard_map/all_to_all | solution.py:24
  162.9 2.2 %shard_map.76 = (bf16[4,392,128]{2,1,0:T(8,128)(2,1)S(1)}, f32[48,2432]{1,0:T(8,128)S(1)}) custom-call(bf16[512,128]{1,0:T(8,128)(2,1)S(1)} %bitcast.27, s32[1]{0:T(128)} %bitcast.refs_1_, f32[8,256]{1,0:T(8,128)S(1)} %broadcast_in_dim.27.refs_2_, bf16[8,128,1024]{2,1,0:T(8,128)(2,1)S(1)} %all-to-all-done.mat.refs_3_, ...), custom_call_target="tpu_custom_call" | custom-call | tf_op jit(solution)/shard_map/pallas_call | solution.py:408
  165.2 15.1 %all_to_all.60.refs_0_ = bf16[4,392,128]{2,1,0:T(8,128)(2,1)S(1)} all-to-all(bf16[4,392,128]{2,1,0:T(8,128)(2,1)S(1)} %get-tuple-element.34), channel_id=1, replica_groups=mesh['zh'=4,'zl'=2,'y'=4,'x'=4,'c'=2] {'zh'}, dimensions={0} | all-to-all | bytes 802816 | tf_op jit(solution)/shard_map/all_to_all | solution.py:24
  180.2 2.0 shard_map.77
  182.2 15.1 %all_to_all.61.pieces = bf16[64,8,128]{2,1,0:T(8,128)(2,1)S(1)} all-to-all(bf16[64,8,128]{2,1,0:T(8,128)(2,1)S(1)} %bitcast.28), channel_id=1, replica_groups=mesh['zh'=4,'zl'=2,'y'=4,'x'=4,'c'=2] {'zl','y','x','c'}, dimensions={0} | all-to-all | bytes 262144 | tf_op jit(solution)/shard_map/all_to_all | solution.py:24
  197.3 0.1 shard_map.78
  197.4 12.6 %all_to_all.62 = bf16[64,8,128]{2,1,0:T(8,128)(2,1)S(1)} all-to-all(bf16[64,8,128]{2,1,0:T(8,128)(2,1)S(1)} %shard_map.78), channel_id=1, replica_groups=mesh['zh'=4,'zl'=2,'y'=4,'x'=4,'c'=2] {'zl','y','x','c'}, dimensions={0} | all-to-all | bytes 262144 | tf_op jit(solution)/shard_map/all_to_all | solution.py:24
  210.0 2.3 %shard_map.79 = (bf16[4,104,128]{2,1,0:T(8,128)(2,1)S(1)}, f32[48,896]{1,0:T(8,128)S(1)}) custom-call(bf16[512,128]{1,0:T(8,128)(2,1)S(1)} %bitcast.26, s32[1]{0:T(128)} %bitcast.refs_1_, f32[8,256]{1,0:T(8,128)S(1)} %broadcast_in_dim.27.refs_2_, bf16[8,128,1024]{2,1,0:T(8,128)(2,1)S(1)} %all-to-all-done.mat.refs_3_, ...), custom_call_target="tpu_custom_call" | custom-call | tf_op jit(solution)/shard_map/pallas_call | solution.py:408
  212.3 9.5 %all_to_all.63.arrived = bf16[4,104,128]{2,1,0:T(8,128)(2,1)S(1)} all-to-all(bf16[4,104,128]{2,1,0:T(8,128)(2,1)S(1)} %get-tuple-element.40), channel_id=1, replica_groups=mesh['zh'=4,'zl'=2,'y'=4,'x'=4,'c'=2] {'zh'}, dimensions={0} | all-to-all | bytes 212992 | tf_op jit(solution)/shard_map/all_to_all | solution.py:24
  221.8 0.9 shard_map.80
  (14 shorter events, 0.1 us)
Async XLA Ops:
  3.1 6.6 %copy-start = (bf16[128,48]{0,1:T(8,128)(2,1)S(1)}, bf16[128,48]{0,1:T(8,128)(2,1)}, u32[]{:S(2)}) copy-start(bf16[128,48]{0,1:T(8,128)(2,1)} %param.6) | copy-start | bytes 36868
  3.1 33.9 %copy-start.1 = (f32[256,256]{1,0:T(8,128)S(1)}, f32[256,256]{1,0:T(8,128)}, u32[]{:S(2)}) copy-start(f32[256,256]{1,0:T(8,128)} %param.7) | copy-start | bytes 786436
  3.1 33.9 %copy-start.2 = (f32[256]{0:T(256)S(1)}, f32[256]{0:T(256)}, u32[]{:S(2)}) copy-start(f32[256]{0:T(256)} %param.8) | copy-start | bytes 3076
  3.1 33.9 %copy-start.3 = (f32[48]{0:T(128)S(1)}, f32[48]{0:T(128)}, u32[]{:S(2)}) copy-start(f32[48]{0:T(128)} %param.9) | copy-start | bytes 580
  3.2 42.4 %all-to-all-start = ((bf16[8,128,1024]{2,1,0:T(8,128)(2,1)}), bf16[8,128,1024]{2,1,0:T(8,128)(2,1)S(1)}, u32[]{:S(2)}, u32[]{:S(2)}) async-start(bf16[8,128,1024]{2,1,0:T(8,128)(2,1)} %shard_map.68), calls=%async_computation | async-start | bytes 4194304 | tf_op jit(solution)/shard_map/all_to_all | solution.py:24
  9.7 24.6 %collective-permute-start.6 = (bf16[48,128]{1,0:T(8,128)(2,1)S(1)}, bf16[48,128]{1,0:T(8,128)(2,1)S(1)}, u32[]{:S(2)}, u32[]{:S(2)}) collective-permute-start(bf16[48,128]{1,0:T(8,128)(2,1)S(1)} %bitcast.30), channel_id=1, source_target_pairs={{0,56},{8,0},{16,8},{24,16},{32,24},{40,32},{48,40},{56,48},{1,57}... | collective-permute-start | bytes 36872 | tf_op jit(solution)/shard_map/ppermute | solution.py:484
  13.2 23.5 %collective-permute-start.5 = (bf16[48,128]{1,0:T(8,128)(2,1)S(1)}, bf16[48,128]{1,0:T(8,128)(2,1)S(1)}, u32[]{:S(2)}, u32[]{:S(2)}) collective-permute-start(bf16[48,128]{1,0:T(8,128)(2,1)S(1)} %bitcast.31), channel_id=1, source_target_pairs={{0,48},{8,56},{16,0},{24,8},{32,16},{40,24},{48,32},{56,40},{1,49}... | collective-permute-start | bytes 36872 | tf_op jit(solution)/shard_map/ppermute | solution.py:484
  13.8 23.3 %collective-permute-start.4 = (bf16[48,128]{1,0:T(8,128)(2,1)S(1)}, bf16[48,128]{1,0:T(8,128)(2,1)S(1)}, u32[]{:S(2)}, u32[]{:S(2)}) collective-permute-start(bf16[48,128]{1,0:T(8,128)(2,1)S(1)} %bitcast.32), channel_id=1, source_target_pairs={{0,40},{8,48},{16,56},{24,0},{32,8},{40,16},{48,24},{56,32},{1,41}... | collective-permute-start | bytes 36872 | tf_op jit(solution)/shard_map/ppermute | solution.py:484
  14.4 27.9 %collective-permute-start.3 = (bf16[48,128]{1,0:T(8,128)(2,1)S(1)}, bf16[48,128]{1,0:T(8,128)(2,1)S(1)}, u32[]{:S(2)}, u32[]{:S(2)}) collective-permute-start(bf16[48,128]{1,0:T(8,128)(2,1)S(1)} %bitcast.33), channel_id=1, source_target_pairs={{0,32},{8,40},{16,48},{24,56},{32,0},{40,8},{48,16},{56,24},{1,33}... | collective-permute-start | bytes 36872 | tf_op jit(solution)/shard_map/ppermute | solution.py:484
  15.6 27.9 %collective-permute-start.2 = (bf16[48,128]{1,0:T(8,128)(2,1)S(1)}, bf16[48,128]{1,0:T(8,128)(2,1)S(1)}, u32[]{:S(2)}, u32[]{:S(2)}) collective-permute-start(bf16[48,128]{1,0:T(8,128)(2,1)S(1)} %bitcast.34), channel_id=1, source_target_pairs={{0,24},{8,32},{16,40},{24,48},{32,56},{40,0},{48,8},{56,16},{1,25}... | collective-permute-start | bytes 36872 | tf_op jit(solution)/shard_map/ppermute | solution.py:484
  34.3 11.3 %collective-permute-start.1 = (bf16[48,128]{1,0:T(8,128)(2,1)S(1)}, bf16[48,128]{1,0:T(8,128)(2,1)S(1)}, u32[]{:S(2)}, u32[]{:S(2)}) collective-permute-start(bf16[48,128]{1,0:T(8,128)(2,1)S(1)} %bitcast.35), channel_id=1, source_target_pairs={{0,16},{8,24},{16,32},{24,40},{32,48},{40,56},{48,0},{56,8},{1,17}... | collective-permute-start | bytes 36872 | tf_op jit(solution)/shard_map/ppermute | solution.py:484
  36.7 8.9 %collective-permute-start = (bf16[48,128]{1,0:T(8,128)(2,1)S(1)}, bf16[48,128]{1,0:T(8,128)(2,1)S(1)}, u32[]{:S(2)}, u32[]{:S(2)}) collective-permute-start(bf16[48,128]{1,0:T(8,128)(2,1)S(1)} %bitcast.36), channel_id=1, source_target_pairs={{0,8},{8,16},{16,24},{24,32},{32,40},{40,48},{48,56},{56,0},{1,9},... | collective-permute-start | bytes 36872 | tf_op jit(solution)/shard_map/ppermute | solution.py:484
  37.1 15.6 %collective-permute-start.9 = (bf16[256,256]{1,0:T(8,128)(2,1)S(1)}, bf16[256,256]{1,0:T(8,128)(2,1)S(1)}, u32[]{:S(2)}, u32[]{:S(2)}) collective-permute-start(bf16[256,256]{1,0:T(8,128)(2,1)S(1)} %convert_element_type.3), channel_id=1, source_target_pairs={{0,192},{64,0},{128,64},{192,128},{1,193},{65,1},{129,65},{193,129... | collective-permute-start | bytes 393224 | tf_op jit(solution)/shard_map/ppermute | solution.py:476
  42.3 10.4 %collective-permute-start.8 = (bf16[256,256]{1,0:T(8,128)(2,1)S(1)}, bf16[256,256]{1,0:T(8,128)(2,1)S(1)}, u32[]{:S(2)}, u32[]{:S(2)}) collective-permute-start(bf16[256,256]{1,0:T(8,128)(2,1)S(1)} %convert_element_type.3), channel_id=1, source_target_pairs={{0,128},{64,192},{128,0},{192,64},{1,129},{65,193},{129,1},{193,65... | collective-permute-start | bytes 393224 | tf_op jit(solution)/shard_map/ppermute | solution.py:476
  43.5 9.2 %collective-permute-start.7 = (bf16[256,256]{1,0:T(8,128)(2,1)S(1)}, bf16[256,256]{1,0:T(8,128)(2,1)S(1)}, u32[]{:S(2)}, u32[]{:S(2)}) collective-permute-start(bf16[256,256]{1,0:T(8,128)(2,1)S(1)} %convert_element_type.3), channel_id=1, source_target_pairs={{0,64},{64,128},{128,192},{192,0},{1,65},{65,129},{129,193},{193,1... | collective-permute-start | bytes 393224 | tf_op jit(solution)/shard_map/ppermute | solution.py:476
  46.8 16.4 %all-to-all-start.1 = ((bf16[4,48,1280]{2,1,0:T(8,128)(2,1)}), bf16[4,48,1280]{2,1,0:T(8,128)(2,1)}, u32[]{:S(2)}, u32[]{:S(2)}) async-start(bf16[4,48,1280]{2,1,0:T(8,128)(2,1)} %shard_map.69), calls=%async_computation.1 | async-start | bytes 983040 | tf_op jit(solution)/shard_map/all_to_all | solution.py:24

commit v4 on v2

--- a/solution.py
+++ b/solution.py
@@ -85,7 +85,7 @@
 CHUNKS, DEEP = 4, 32
 
 
-def pack_kernel(design, goal, out, rows, packed, goals, sems):
+def pack_kernel(design, goal_in, out, rows, packed, goals, goal, sems):
     def inward(index):
         at = pl.ds(index * DEEP, DEEP)
         return pltpu.make_async_copy(design.at[at, :], rows.at[at, :], sems.at[index])
@@ -98,14 +98,18 @@
 
     for index in range(CHUNKS):
         inward(index).start()
-    for to in range(8):
-        for index in range(6):
-            goals[to, :, index * 128 : (index + 1) * 128] = goal[index * 8 : index * 8 + 8, :]
-        goals[to, :, 768:] = jnp.zeros((8, 256), BF)
+    fetched = pltpu.make_async_copy(goal_in, goal, sems.at[2 * CHUNKS + 1])
+    fetched.start()
     last = pltpu.make_async_copy(goals, out.at[:, 128:136, :], sems.at[2 * CHUNKS])
-    last.start()
     for index in range(CHUNKS):
         inward(index).wait()
+        if index == 1:
+            fetched.wait()
+            for to in range(8):
+                for at in range(6):
+                    goals[to, :, at * 128 : (at + 1) * 128] = goal[at * 8 : at * 8 + 8, :]
+                goals[to, :, 768:] = jnp.zeros((8, 256), BF)
+            last.start()
         low, high = index * DEEP, (index + 1) * DEEP
         for to in range(8):
             for part in range(4):
@@ -121,13 +125,14 @@
     return pl.pallas_call(
         pack_kernel,
         out_shape=shape(8, 136, BLOCK, dtype=BF),
-        in_specs=[IN_HBM, IN_VMEM],
+        in_specs=[IN_HBM, IN_HBM],
         out_specs=IN_HBM,
         scratch_shapes=[
             pltpu.VMEM((128, 8192), BF),
             pltpu.VMEM((8, 128, BLOCK), BF),
             pltpu.VMEM((8, 8, BLOCK), BF),
-            pltpu.SemaphoreType.DMA((2 * CHUNKS + 1,)),
+            pltpu.VMEM((T, 128), BF),
+            pltpu.SemaphoreType.DMA((2 * CHUNKS + 2,)),
         ],
     )(design, goal)
 

time: 216 us -> 215 us (level)
  no operation moved by 1% of the time
where the time goes in v4:
time: 215 us
  blocking collectives  140 us (65%)
  waiting for transfers between devices  33.2 us (15%)
  starting transfers between devices  22.5 us (10%)
  Pallas kernels  18.3 us (9%)
    all_to_all x9, blocking collectives, exchange(): return lax.all_to_all(pieces, axes, 0, 0, tiled=True)  140 us
    all_to_all x2, waiting for transfers between devices, exchange(): return lax.all_to_all(pieces, axes, 0, 0, tiled=True)  30 us
    all_to_all x2, starting transfers between devices, exchange(): return lax.all_to_all(pieces, axes, 0, 0, tiled=True)  14.2 us
    ppermute x3, starting transfers between devices, program(): other = lax.ppermute(low_factor, 'zh', pairs)  8.4 us
    pallas_call x3, Pallas kernels, search_call(): pl.pallas_call(lambda *refs: search_kernel(first, last, *refs), out_shape...  6.2 us
  transfers between devices with their start and end apart: 5, of which 3 were waited for; matrix products, arithmetic and copies ran while one was open for 0% of the time, Pallas kernels for 1%

profile of v4, /device:TPU:1, one launch (start us, length us, event | category | flops | bytes accessed | tf_op | source)
XLA Modules:
  0.0 214.8 jit_solution(259367554818175008)
XLA Ops:
  0.6 2.8 %shard_map.68 = bf16[8,136,1024]{2,1,0:T(8,128)(2,1)} custom-call(bf16[128,8192]{1,0:T(8,128)(2,1)} %design.1, bf16[48,128]{1,0:T(8,128)(2,1)} %bitcast.29), custom_call_target="tpu_custom_call" | custom-call | tf_op jit(solution)/shard_map/pallas_call | solution.py:125
  3.4 0.0 copy-start
  3.4 0.0 copy-start.1
  3.4 0.0 copy-start.2
  3.4 6.5 %all-to-all-start = ((bf16[8,136,1024]{2,1,0:T(8,128)(2,1)}), bf16[8,136,1024]{2,1,0:T(8,128)(2,1)S(1)}, u32[]{:S(2)}, u32[]{:S(2)}) async-start(bf16[8,136,1024]{2,1,0:T(8,128)(2,1)} %shard_map.68), calls=%async_computation | async-start | bytes 4456448 | tf_op jit(solution)/shard_map/all_to_all | solution.py:24
  9.9 0.0 copy-done
  10.0 0.0 copy-done.1
  10.0 0.0 copy-done.2
  10.0 0.1 broadcast_in_dim.29.refs_2_.penalty
  10.1 5.1 %collective-permute-start.2 = (bf16[256,256]{1,0:T(8,128)(2,1)S(1)}, bf16[256,256]{1,0:T(8,128)(2,1)S(1)}, u32[]{:S(2)}, u32[]{:S(2)}) collective-permute-start(bf16[256,256]{1,0:T(8,128)(2,1)S(1)} %convert_element_type.3), channel_id=1, source_target_pairs={{0,192},{64,0},{128,64},{192,128},{1,193},{65,1},{129,65},{193,129... | collective-permute-start | bytes 393224 | tf_op jit(solution)/shard_map/ppermute | solution.py:480
  15.2 1.2 collective-permute-start.1
  16.4 2.1 collective-permute-start
  18.5 19.8 %all-to-all-done.mat.refs_3_ = bf16[8,136,1024]{2,1,0:T(8,128)(2,1)S(1)} async-done(((bf16[8,136,1024]{2,1,0:T(8,128)(2,1)}), bf16[8,136,1024]{2,1,0:T(8,128)(2,1)S(1)}, u32[]{:S(2)}, u32[]{:S(2)}) %all-to-all-start) | async-done | bytes 2228256 | tf_op jit(solution)/shard_map/all_to_all | solution.py:24
  38.3 1.2 shard_map.69
  39.5 7.6 %all-to-all-start.1 = ((bf16[4,48,1280]{2,1,0:T(8,128)(2,1)}), bf16[4,48,1280]{2,1,0:T(8,128)(2,1)}, u32[]{:S(2)}, u32[]{:S(2)}) async-start(bf16[4,48,1280]{2,1,0:T(8,128)(2,1)} %shard_map.69), calls=%async_computation.1 | async-start | bytes 983040 | tf_op jit(solution)/shard_map/all_to_all | solution.py:24
  47.3 3.2 %collective-permute-done = bf16[256,256]{1,0:T(8,128)(2,1)S(1)} collective-permute-done((bf16[256,256]{1,0:T(8,128)(2,1)S(1)}, bf16[256,256]{1,0:T(8,128)(2,1)S(1)}, u32[]{:S(2)}, u32[]{:S(2)}) %collective-permute-start) | collective-permute-done | bytes 131104 | tf_op jit(solution)/shard_map/ppermute | solution.py:480
  50.5 0.0 collective-permute-done.1
  50.5 0.0 collective-permute-done.2
  50.5 0.9 shard_map.70.cross
  51.4 10.2 %all-to-all-done.1.arrived = bf16[4,48,1280]{2,1,0:T(8,128)(2,1)} async-done(((bf16[4,48,1280]{2,1,0:T(8,128)(2,1)}), bf16[4,48,1280]{2,1,0:T(8,128)(2,1)}, u32[]{:S(2)}, u32[]{:S(2)}) %all-to-all-start.1) | async-done | bytes 491552 | tf_op jit(solution)/shard_map/all_to_all | solution.py:24
  61.6 2.3 %shard_map.71 = (bf16[64,48,128]{2,1,0:T(8,128)(2,1)S(1)}, f32[48,1280]{1,0:T(8,128)S(1)}) custom-call(bf16[4,48,1280]{2,1,0:T(8,128)(2,1)} %all-to-all-done.1.arrived, bf16[8,136,1024]{2,1,0:T(8,128)(2,1)S(1)} %all-to-all-done.mat.refs_3_, bf16[1024,256]{1,0:T(8,128)(2,1)S(1)} %bitcast.19, bf16[64,40,128]{2,1,0:T(8,128)(2,1)S(1)} %shard_map.70.cross), custom_call_target="tpu_custom_call" | custom-call | tf_op jit(solution)/shard_map/pallas_call | solution.py:207
  63.9 24.6 %all_to_all.55.pieces = bf16[64,48,128]{2,1,0:T(8,128)(2,1)S(1)} all-to-all(bf16[64,48,128]{2,1,0:T(8,128)(2,1)S(1)} %get-tuple-element.23), channel_id=1, replica_groups=mesh['zh'=4,'zl'=2,'y'=4,'x'=4,'c'=2] {'zl','y','x','c'}, dimensions={0} | all-to-all | bytes 1572864 | tf_op jit(solution)/shard_map/all_to_all | solution.py:24
  88.5 0.2 shard_map.72
  88.7 19.4 %all_to_all.56.refs_0_.refs_7_ = bf16[64,48,128]{2,1,0:T(8,128)(2,1)S(1)} all-to-all(bf16[64,48,128]{2,1,0:T(8,128)(2,1)S(1)} %shard_map.72), channel_id=1, replica_groups=mesh['zh'=4,'zl'=2,'y'=4,'x'=4,'c'=2] {'zl','y','x','c'}, dimensions={0} | all-to-all | bytes 1572864 | tf_op jit(solution)/shard_map/all_to_all | solution.py:24
  108.1 1.7 shard_map.73
  109.8 16.0 %all_to_all.57.refs_0_ = bf16[4,392,128]{2,1,0:T(8,128)(2,1)S(1)} all-to-all(bf16[4,392,128]{2,1,0:T(8,128)(2,1)S(1)} %get-tuple-element.27), channel_id=1, replica_groups=mesh['zh'=4,'zl'=2,'y'=4,'x'=4,'c'=2] {'zh'}, dimensions={0} | all-to-all | bytes 802816 | tf_op jit(solution)/shard_map/all_to_all | solution.py:24
  125.8 1.7 shard_map.74
  127.5 14.6 %all_to_all.58.pieces = bf16[64,8,128]{2,1,0:T(8,128)(2,1)S(1)} all-to-all(bf16[64,8,128]{2,1,0:T(8,128)(2,1)S(1)} %bitcast.28), channel_id=1, replica_groups=mesh['zh'=4,'zl'=2,'y'=4,'x'=4,'c'=2] {'zl','y','x','c'}, dimensions={0} | all-to-all | bytes 262144 | tf_op jit(solution)/shard_map/all_to_all | solution.py:24
  142.1 0.1 shard_map.75
  142.2 12.6 %all_to_all.59 = bf16[64,8,128]{2,1,0:T(8,128)(2,1)S(1)} all-to-all(bf16[64,8,128]{2,1,0:T(8,128)(2,1)S(1)} %shard_map.75), channel_id=1, replica_groups=mesh['zh'=4,'zl'=2,'y'=4,'x'=4,'c'=2] {'zl','y','x','c'}, dimensions={0} | all-to-all | bytes 262144 | tf_op jit(solution)/shard_map/all_to_all | solution.py:24
  154.8 2.2 %shard_map.76 = (bf16[4,392,128]{2,1,0:T(8,128)(2,1)S(1)}, f32[48,2432]{1,0:T(8,128)S(1)}) custom-call(bf16[512,128]{1,0:T(8,128)(2,1)S(1)} %bitcast.26, s32[1]{0:T(128)} %bitcast.1.refs_1_, f32[8,256]{1,0:T(8,128)S(1)} %broadcast_in_dim.28.refs_2_, bf16[8,136,1024]{2,1,0:T(8,128)(2,1)S(1)} %all-to-all-done.mat.refs_3_, ...), custom_call_target="tpu_custom_call" | custom-call | tf_op jit(solution)/shard_map/pallas_call | solution.py:413
  157.1 15.1 %all_to_all.60.refs_0_ = bf16[4,392,128]{2,1,0:T(8,128)(2,1)S(1)} all-to-all(bf16[4,392,128]{2,1,0:T(8,128)(2,1)S(1)} %get-tuple-element.32), channel_id=1, replica_groups=mesh['zh'=4,'zl'=2,'y'=4,'x'=4,'c'=2] {'zh'}, dimensions={0} | all-to-all | bytes 802816 | tf_op jit(solution)/shard_map/all_to_all | solution.py:24
  172.2 2.0 shard_map.77
  174.2 15.2 %all_to_all.61.pieces = bf16[64,8,128]{2,1,0:T(8,128)(2,1)S(1)} all-to-all(bf16[64,8,128]{2,1,0:T(8,128)(2,1)S(1)} %bitcast.27), channel_id=1, replica_groups=mesh['zh'=4,'zl'=2,'y'=4,'x'=4,'c'=2] {'zl','y','x','c'}, dimensions={0} | all-to-all | bytes 262144 | tf_op jit(solution)/shard_map/all_to_all | solution.py:24
  189.4 0.1 shard_map.78
  189.5 12.6 %all_to_all.62 = bf16[64,8,128]{2,1,0:T(8,128)(2,1)S(1)} all-to-all(bf16[64,8,128]{2,1,0:T(8,128)(2,1)S(1)} %shard_map.78), channel_id=1, replica_groups=mesh['zh'=4,'zl'=2,'y'=4,'x'=4,'c'=2] {'zl','y','x','c'}, dimensions={0} | all-to-all | bytes 262144 | tf_op jit(solution)/shard_map/all_to_all | solution.py:24
  202.1 2.3 %shard_map.79 = (bf16[4,104,128]{2,1,0:T(8,128)(2,1)S(1)}, f32[48,896]{1,0:T(8,128)S(1)}) custom-call(bf16[512,128]{1,0:T(8,128)(2,1)S(1)} %bitcast.25, s32[1]{0:T(128)} %bitcast.1.refs_1_, f32[8,256]{1,0:T(8,128)S(1)} %broadcast_in_dim.28.refs_2_, bf16[8,136,1024]{2,1,0:T(8,128)(2,1)S(1)} %all-to-all-done.mat.refs_3_, ...), custom_call_target="tpu_custom_call" | custom-call | tf_op jit(solution)/shard_map/pallas_call | solution.py:413
  204.4 9.5 %all_to_all.63.arrived = bf16[4,104,128]{2,1,0:T(8,128)(2,1)S(1)} all-to-all(bf16[4,104,128]{2,1,0:T(8,128)(2,1)S(1)} %get-tuple-element.38), channel_id=1, replica_groups=mesh['zh'=4,'zl'=2,'y'=4,'x'=4,'c'=2] {'zh'}, dimensions={0} | all-to-all | bytes 212992 | tf_op jit(solution)/shard_map/all_to_all | solution.py:24
  213.9 0.9 shard_map.80
  (7 shorter events, 0.1 us)
Async XLA Ops:
  3.4 6.5 %copy-start = (f32[256,256]{1,0:T(8,128)S(1)}, f32[256,256]{1,0:T(8,128)}, u32[]{:S(2)}) copy-start(f32[256,256]{1,0:T(8,128)} %param.7) | copy-start | bytes 786436
  3.4 6.6 %copy-start.1 = (f32[256]{0:T(256)S(1)}, f32[256]{0:T(256)}, u32[]{:S(2)}) copy-start(f32[256]{0:T(256)} %param.8) | copy-start | bytes 3076
  3.4 6.6 %copy-start.2 = (f32[48]{0:T(128)S(1)}, f32[48]{0:T(128)}, u32[]{:S(2)}) copy-start(f32[48]{0:T(128)} %param.9) | copy-start | bytes 580
  3.4 34.9 %all-to-all-start = ((bf16[8,136,1024]{2,1,0:T(8,128)(2,1)}), bf16[8,136,1024]{2,1,0:T(8,128)(2,1)S(1)}, u32[]{:S(2)}, u32[]{:S(2)}) async-start(bf16[8,136,1024]{2,1,0:T(8,128)(2,1)} %shard_map.68), calls=%async_computation | async-start | bytes 4456448 | tf_op jit(solution)/shard_map/all_to_all | solution.py:24
  10.1 40.4 %collective-permute-start.2 = (bf16[256,256]{1,0:T(8,128)(2,1)S(1)}, bf16[256,256]{1,0:T(8,128)(2,1)S(1)}, u32[]{:S(2)}, u32[]{:S(2)}) collective-permute-start(bf16[256,256]{1,0:T(8,128)(2,1)S(1)} %convert_element_type.3), channel_id=1, source_target_pairs={{0,192},{64,0},{128,64},{192,128},{1,193},{65,1},{129,65},{193,129... | collective-permute-start | bytes 393224 | tf_op jit(solution)/shard_map/ppermute | solution.py:480
  15.2 35.2 %collective-permute-start.1 = (bf16[256,256]{1,0:T(8,128)(2,1)S(1)}, bf16[256,256]{1,0:T(8,128)(2,1)S(1)}, u32[]{:S(2)}, u32[]{:S(2)}) collective-permute-start(bf16[256,256]{1,0:T(8,128)(2,1)S(1)} %convert_element_type.3), channel_id=1, source_target_pairs={{0,128},{64,192},{128,0},{192,64},{1,129},{65,193},{129,1},{193,65... | collective-permute-start | bytes 393224 | tf_op jit(solution)/shard_map/ppermute | solution.py:480
  16.4 34.1 %collective-permute-start = (bf16[256,256]{1,0:T(8,128)(2,1)S(1)}, bf16[256,256]{1,0:T(8,128)(2,1)S(1)}, u32[]{:S(2)}, u32[]{:S(2)}) collective-permute-start(bf16[256,256]{1,0:T(8,128)(2,1)S(1)} %convert_element_type.3), channel_id=1, source_target_pairs={{0,64},{64,128},{128,192},{192,0},{1,65},{65,129},{129,193},{193,1... | collective-permute-start | bytes 393224 | tf_op jit(solution)/shard_map/ppermute | solution.py:480
  39.5 22.1 %all-to-all-start.1 = ((bf16[4,48,1280]{2,1,0:T(8,128)(2,1)}), bf16[4,48,1280]{2,1,0:T(8,128)(2,1)}, u32[]{:S(2)}, u32[]{:S(2)}) async-start(bf16[4,48,1280]{2,1,0:T(8,128)(2,1)} %shard_map.69), calls=%async_computation.1 | async-start | bytes 983040 | tf_op jit(solution)/shard_map/all_to_all | solution.py:24
